TPU v7x, 128 devices: a whole 4x4x4 slice. The times are simulated.
128 devices in a mesh: sp: 16 (over z, y), dp: 8 (over x, core).
Axes of the slice: x: 4, y: 4, z: 4, core: 2. Of those that a mesh axis runs over, the one named last changes fastest.
Arguments:
- node_lat: bfloat16 [32, 4096, 256], P('dp', 'sp')
- edge_lat: bfloat16 [32, 24576, 256], P('dp', 'sp')
- senders: int32 [24576], P('sp')
- edge_mask: int32 [24576], P('sp')
- node_cot: bfloat16 [32, 4096, 256], P('dp', 'sp')
- edge_cot: bfloat16 [32, 24576, 256], P('dp', 'sp')
- w_edge1: float32 [2, 768, 256], P(None, 'dp')
- w_edge2: float32 [2, 256, 256], P(None, 'dp')
- w_node1: float32 [2, 512, 256], P(None, 'dp')
- w_node2: float32 [2, 256, 256], P(None, 'dp')
- norm_par: float32 [2, 4, 256], P(None, None, 'dp')
- mom_edge1: float32 [2, 768, 256], P(None, 'dp')
- mom_edge2: float32 [2, 256, 256], P(None, 'dp')
- mom_node1: float32 [2, 512, 256], P(None, 'dp')
- mom_node2: float32 [2, 256, 256], P(None, 'dp')
- mom_norm: float32 [2, 4, 256], P(None, None, 'dp')
- vel_edge1: float32 [2, 768, 256], P(None, 'dp')
- vel_edge2: float32 [2, 256, 256], P(None, 'dp')
- vel_node1: float32 [2, 512, 256], P(None, 'dp')
- vel_node2: float32 [2, 256, 256], P(None, 'dp')
- vel_norm: float32 [2, 4, 256], P(None, None, 'dp')
Outputs:
- output 1: float32 [2, 768, 256], P(None, 'dp')
- output 2: float32 [2, 256, 256], P(None, 'dp')
- output 3: float32 [2, 512, 256], P(None, 'dp')
- output 4: float32 [2, 256, 256], P(None, 'dp')
- output 5: float32 [2, 4, 256], P(None, None, 'dp')
- output 6: float32 [2, 768, 256], P(None, 'dp')
- output 7: float32 [2, 256, 256], P(None, 'dp')
- output 8: float32 [2, 512, 256], P(None, 'dp')
- output 9: float32 [2, 256, 256], P(None, 'dp')
- output 10: float32 [2, 4, 256], P(None, None, 'dp')
- output 11: float32 [2, 768, 256], P(None, 'dp')
- output 12: float32 [2, 256, 256], P(None, 'dp')
- output 13: float32 [2, 512, 256], P(None, 'dp')
- output 14: float32 [2, 256, 256], P(None, 'dp')
- output 15: float32 [2, 4, 256], P(None, None, 'dp')
- output 16: bfloat16 [32, 4096, 256], P('dp', 'sp')
- output 17: bfloat16 [32, 24576, 256], P('dp', 'sp')
All inputs are finite; a program needn't handle non-finite values.
Results may differ from a plain program's by a relative error of at most 0.02.
Values are sent between devices in bfloat16 or wider.
A program may use at most 1 GiB of HBM per device.

v0:
```python
import functools

import jax
import jax.numpy as jnp
from jax import lax
from jax.experimental import pallas as pl
from jax.experimental.layout import Layout, with_layout_constraint
from jax.experimental.pallas import tpu as pltpu
from jax.sharding import PartitionSpec as P

NORM_EPS = 1e-5
LEARN_RATE = 1e-3
BETA_ONE = 0.9
BETA_TWO = 0.95
ADAM_EPS = 1e-8
DECAY = 0.1
STEP = 10

BF = jnp.bfloat16
F32 = jnp.float32
SLOTS = 80
MESH_ID = pl.DeviceIdType.MESH


def ring_gap(offset, count):
    return min(offset % count, -offset % count)


def far_first(tiles):
    side = int(tiles ** 0.5)
    return sorted(range(1, tiles), key=lambda offset: -ring_gap(offset // side, side) - ring_gap(offset, side))


def line_first(count):
    return sorted(range(1, count), key=lambda offset: -ring_gap(offset, count))

LANES = 128
SHARD_ROWS = (96, 32, 64, 32)
SHARD_OFF = (0, 96, 128, 192)
NORM_OFF = 224
PART_ROWS = 240
FULL_ROWS = 256
GRAD_ROWS = 1800


def contract(left_op, right_op, left_dims, right_dims):
    return lax.dot_general(left_op, right_op, ((left_dims, right_dims), ((), ())), preferred_element_type=jnp.float32)


def norm_forward(out_b, norm_gain, norm_bias):
    values = out_b.astype(jnp.float32)
    centered = values - jnp.mean(values, axis=-1, keepdims=True)
    inv_std = lax.rsqrt(jnp.mean(centered * centered, axis=-1, keepdims=True) + NORM_EPS)
    normed = centered * inv_std
    return normed * norm_gain + norm_bias, normed, inv_std


def mlp_tail(pre_act, w_two, norm_gain, norm_bias):
    pre_b = pre_act.astype(jnp.bfloat16)
    hidden_act = jax.nn.silu(pre_b.astype(jnp.float32)).astype(jnp.bfloat16)
    last_dim = hidden_act.ndim - 1
    out_b = contract(hidden_act, w_two, (last_dim,), (0,)).astype(jnp.bfloat16)
    branch, normed, inv_std = norm_forward(out_b, norm_gain, norm_bias)
    return branch, (pre_b, hidden_act, normed, inv_std)


def mlp_back(d_branch, saved, w_one, w_two, norm_gain):
    pre_b, hidden_act, normed, inv_std = saved
    last_dim = hidden_act.ndim - 1
    lead_dims = tuple(range(last_dim))
    d_gain = jnp.sum(d_branch * normed, axis=lead_dims)
    d_bias = jnp.sum(d_branch, axis=lead_dims)
    d_norm = d_branch * norm_gain
    d_out = (inv_std * (d_norm - jnp.mean(d_norm, axis=-1, keepdims=True) - normed * jnp.mean(d_norm * normed, axis=-1, keepdims=True))).astype(jnp.bfloat16)
    d_two = contract(hidden_act, d_out, lead_dims, lead_dims)
    d_act = contract(d_out, w_two, (last_dim,), (1,)).astype(jnp.bfloat16)
    pre_f = pre_b.astype(jnp.float32)
    gate_sig = jax.nn.sigmoid(pre_f)
    d_pre = (d_act.astype(jnp.float32) * gate_sig * (1.0 + pre_f * (1.0 - gate_sig))).astype(jnp.bfloat16)
    d_in = contract(d_pre, w_one, (last_dim,), (1,))
    return d_pre, d_in, d_two, d_gain, d_bias


def layer_forward(node_x, node_all, edge_x, senders, mask_b, layer_wts):
    w_e1, w_e2, w_n1, w_n2, norm_rows = layer_wts
    lat_width = node_x.shape[-1]
    sender_lat = jnp.take(node_all, senders, axis=1).reshape(edge_x.shape)
    pre_e = (contract(edge_x, w_e1[:lat_width], (3,), (0,))
             + contract(sender_lat, w_e1[lat_width:2 * lat_width], (3,), (0,))
             + contract(node_x, w_e1[2 * lat_width:], (2,), (0,))[:, :, None, :])
    branch_e, saved_e = mlp_tail(pre_e, w_e2, norm_rows[0], norm_rows[1])
    edge_new = (edge_x.astype(jnp.float32) + branch_e).astype(jnp.bfloat16)
    node_sum = jnp.einsum('bngd,ng->bnd', edge_new, mask_b, preferred_element_type=jnp.float32).astype(jnp.bfloat16)
    pre_n = contract(node_x, w_n1[:lat_width], (2,), (0,)) + contract(node_sum, w_n1[lat_width:], (2,), (0,))
    branch_n, saved_n = mlp_tail(pre_n, w_n2, norm_rows[2], norm_rows[3])
    node_new = (node_x.astype(jnp.float32) + branch_n).astype(jnp.bfloat16)
    return node_new, edge_new, (sender_lat, node_sum, saved_e, saved_n)


def layer_backward(d_node_new, d_edge_new, node_x, edge_x, senders, mask_f, saved, layer_wts, total_nodes):
    w_e1, w_e2, w_n1, w_n2, norm_rows = layer_wts
    sender_lat, node_sum, saved_e, saved_n = saved
    batch_size, tile_nodes, degree, lat_width = edge_x.shape
    d_res_n = d_node_new.astype(jnp.float32)
    d_pre_n, d_in_n, d_wn2, d_gain_n, d_bias_n = mlp_back(d_res_n, saved_n, w_n1, w_n2, norm_rows[2])
    d_wn1 = jnp.concatenate([contract(node_x, d_pre_n, (0, 1), (0, 1)), contract(node_sum, d_pre_n, (0, 1), (0, 1))], axis=0)
    d_sum = d_in_n[..., lat_width:].astype(jnp.bfloat16)
    d_res_e = (d_edge_new.astype(jnp.float32) + d_sum.astype(jnp.float32)[:, :, None, :] * mask_f[None, :, :, None]).astype(jnp.bfloat16).astype(jnp.float32)
    d_pre_e, d_in_e, d_we2, d_gain_e, d_bias_e = mlp_back(d_res_e, saved_e, w_e1, w_e2, norm_rows[0])
    recv_grad = contract(node_x, d_pre_e.reshape(batch_size, tile_nodes, -1), (0, 1), (0, 1))
    d_we1 = jnp.concatenate([contract(edge_x, d_pre_e, (0, 1, 2), (0, 1, 2)), contract(sender_lat, d_pre_e, (0, 1, 2), (0, 1, 2)), recv_grad.reshape(lat_width, degree, -1).sum(axis=1)], axis=0)
    d_edge_x = (d_res_e + d_in_e[..., :lat_width]).astype(jnp.bfloat16)
    d_sender = d_in_e[..., lat_width:2 * lat_width].reshape(batch_size, tile_nodes * degree, lat_width)
    scattered = jnp.zeros((batch_size, total_nodes, lat_width), jnp.float32).at[:, senders].add(d_sender)
    d_local = d_res_n + d_in_n[..., :lat_width] + d_in_e[..., 2 * lat_width:].sum(axis=2)
    grads = (d_we1, d_we2, d_wn1, d_wn2, jnp.stack([d_gain_e, d_bias_e, d_gain_n, d_bias_n]))
    return d_local, scattered, d_edge_x, grads


def row_major(value):
    return with_layout_constraint(value, Layout(tuple(range(value.ndim))))


def adamw_update(master, grad_sum, moment_one, moment_two):
    corr_one = 1.0 - BETA_ONE ** STEP
    corr_two = 1.0 - BETA_TWO ** STEP
    one_new = BETA_ONE * moment_one + (1.0 - BETA_ONE) * grad_sum
    two_new = BETA_TWO * moment_two + (1.0 - BETA_TWO) * grad_sum * grad_sum
    direction = (one_new / corr_one) / (jnp.sqrt(two_new / corr_two) + ADAM_EPS)
    return master - LEARN_RATE * (direction + DECAY * master), one_new, two_new


def dot_nn(left_op, right_op):
    return lax.dot_general(left_op, right_op, (((1,), (0,)), ((), ())), preferred_element_type=F32)


def dot_nt(left_op, right_op):
    return lax.dot_general(left_op, right_op, (((1,), (1,)), ((), ())), preferred_element_type=F32)


def dot_tn(left_op, right_op):
    return lax.dot_general(left_op, right_op, (((0,), (0,)), ((), ())), preferred_element_type=F32)


def split_three(values):
    high = values.astype(BF)
    rest = values - high.astype(F32)
    mid = rest.astype(BF)
    low = (rest - mid.astype(F32)).astype(BF)
    return high, mid, low


def to_bf(cond):
    return jnp.where(cond, 1.0, 0.0).astype(BF)


def onehot_cols(col_ids, first, width):
    rows = col_ids.shape[0]
    lane = lax.broadcasted_iota(jnp.int32, (rows, LANES), 1)
    parts = [to_bf(col_ids == lane + (first + LANES * i)) for i in range(width // LANES)]
    return jnp.concatenate(parts, axis=1)


def onehot_rows(row_ids, first, height):
    width = row_ids.shape[1]
    sub = lax.broadcasted_iota(jnp.int32, (height, width), 0) + first
    return to_bf(row_ids == sub)


def norm_parts(out_b):
    values = out_b.astype(F32)
    centered = values - jnp.mean(values, axis=-1, keepdims=True)
    inv_std = lax.rsqrt(jnp.mean(centered * centered, axis=-1, keepdims=True) + NORM_EPS)
    return centered * inv_std, inv_std


def branch_forward(pre_act, w_two, gain, bias):
    pre_b = pre_act.astype(BF)
    pre_f = pre_b.astype(F32)
    sig = jax.nn.sigmoid(pre_f)
    act = (pre_f * sig).astype(BF)
    out_b = dot_nn(act, w_two).astype(BF)
    normed, inv_std = norm_parts(out_b)
    return normed * gain + bias, (pre_b, act, sig, normed, inv_std, out_b)


def branch_backward(d_branch, pre_b, act, sig, normed, inv_std, w_two, gain):
    d_norm = d_branch * gain
    mean_one = jnp.mean(d_norm, axis=-1, keepdims=True)
    mean_two = jnp.mean(d_norm * normed, axis=-1, keepdims=True)
    d_out = (inv_std * (d_norm - mean_one - normed * mean_two)).astype(BF)
    d_two = dot_tn(act, d_out)
    d_act = dot_nt(d_out, w_two).astype(BF)
    pre_f = pre_b.astype(F32)
    d_pre = (d_act.astype(F32) * sig * (1.0 + pre_f * (1.0 - sig))).astype(BF)
    d_gain = jnp.sum(d_branch * normed, axis=0, keepdims=True)
    d_bias = jnp.sum(d_branch, axis=0, keepdims=True)
    return d_pre, d_two, d_gain, d_bias


def load_weights(part_ref, layer, all_wts, norm_ref):
    norm = jnp.zeros((PART_ROWS - NORM_OFF, part_ref.shape[-1]), F32)
    for shard in range(part_ref.shape[0]):
        for ref, rows, off in zip(all_wts, SHARD_ROWS, SHARD_OFF):
            ref[layer, shard * rows:(shard + 1) * rows, :] = part_ref[shard, off:off + rows, :]
        norm += part_ref[shard, NORM_OFF:, :].astype(F32)
    norm_ref[layer] = norm[:8]


def cast_parts(master_refs, part_ref):
    dp = lax.axis_index('dp')
    layers, gains, lanes = master_refs[-1].shape
    width = part_ref.shape[-1]
    spot = lax.broadcasted_iota(jnp.int32, (lanes, width), 1) - lanes * dp
    place = to_bf(spot == lax.broadcasted_iota(jnp.int32, (lanes, width), 0))
    for layer in range(layers):
        for ref, rows, off in zip(master_refs, SHARD_ROWS, SHARD_OFF):
            part_ref[layer, off:off + rows, :] = ref[layer].astype(BF)
        norm = jnp.concatenate([master_refs[-1][layer], jnp.zeros((PART_ROWS - NORM_OFF - gains, lanes), F32)], axis=0)
        part_ref[layer, NORM_OFF:, :] = dot_nn(norm.astype(BF), place).astype(BF)


def peer_tile(me, offset, side):
    row = lax.rem(me // side + offset // side, side)
    col = lax.rem(lax.rem(me, side) + offset % side, side)
    return row * side + col


def greet(peers):
    barrier = pltpu.get_barrier_semaphore()
    for peer in peers:
        pl.semaphore_signal(barrier, inc=1, device_id=peer, device_id_type=MESH_ID)


def greeted(count):
    pl.semaphore_wait(pltpu.get_barrier_semaphore(), count)


def tile_peers(tiles):
    me = lax.axis_index('sp')
    dp = lax.axis_index('dp')
    side = int(tiles ** 0.5)
    return [(peer_tile(me, offset, side), dp) for offset in far_first(tiles)]


def slot_copy(src_ref, dst_ref, sample, spot, send_sem, recv_sem, peer, me):
    return pltpu.make_async_remote_copy(src_ref=src_ref.at[peer[0], sample], dst_ref=dst_ref.at[me, sample], send_sem=send_sem.at[sample, spot], recv_sem=recv_sem.at[sample, spot], device_id=peer, device_id_type=MESH_ID)


def slots_start(src_ref, dst_ref, sample, send_sem, recv_sem, self_sem, tiles):
    me = lax.axis_index('sp')
    pltpu.make_async_copy(src_ref.at[me, sample], dst_ref.at[me, sample], self_sem.at[sample]).start()
    for spot, peer in enumerate(tile_peers(tiles)):
        slot_copy(src_ref, dst_ref, sample, spot, send_sem, recv_sem, peer, me).start()


def slots_wait(src_ref, dst_ref, sample, send_sem, recv_sem, self_sem, tiles):
    me = lax.axis_index('sp')
    pltpu.make_async_copy(src_ref.at[me, sample], dst_ref.at[me, sample], self_sem.at[sample]).wait()
    for spot, peer in enumerate(tile_peers(tiles)):
        slot_copy(src_ref, dst_ref, sample, spot, send_sem, recv_sem, peer, me).wait()


def slots_wait_all(src_ref, dst_ref, samples, send_sem, recv_sem, self_sem, tiles):
    def one(sample, carry):
        slots_wait(src_ref, dst_ref, sample, send_sem, recv_sem, self_sem, tiles)
        return carry
    lax.fori_loop(0, samples, one, 0)


def shard_peers(count):
    me = lax.axis_index('sp')
    dp = lax.axis_index('dp')
    return [(me, lax.rem(dp + offset, count)) for offset in line_first(count)]


def shard_copy(src_ref, dst_ref, spot, send_sem, recv_sem, peer, scatter):
    dp = lax.axis_index('dp')
    src = src_ref.at[peer[1]] if scatter else src_ref
    return pltpu.make_async_remote_copy(src_ref=src, dst_ref=dst_ref.at[dp], send_sem=send_sem.at[spot], recv_sem=recv_sem.at[spot], device_id=peer, device_id_type=MESH_ID)


def shards_start(src_ref, dst_ref, send_sem, recv_sem, self_sem, count, scatter):
    dp = lax.axis_index('dp')
    pltpu.make_async_copy(src_ref.at[dp] if scatter else src_ref, dst_ref.at[dp], self_sem).start()
    for spot, peer in enumerate(shard_peers(count)):
        shard_copy(src_ref, dst_ref, spot, send_sem, recv_sem, peer, scatter).start()


def shards_wait(src_ref, dst_ref, send_sem, recv_sem, self_sem, count, scatter):
    dp = lax.axis_index('dp')
    pltpu.make_async_copy(src_ref.at[dp] if scatter else src_ref, dst_ref.at[dp], self_sem).wait()
    for spot, peer in enumerate(shard_peers(count)):
        shard_copy(src_ref, dst_ref, spot, send_sem, recv_sem, peer, scatter).wait()


def chunk_maps(degree, mask_rows, mask_col):
    chunk = mask_rows.shape[1]
    nodes = chunk // degree
    sub_w = lax.broadcasted_iota(jnp.int32, (nodes, chunk), 0) * degree
    lane_w = lax.broadcasted_iota(jnp.int32, (nodes, chunk), 1)
    wide = (lane_w >= sub_w) & (lane_w < sub_w + degree)
    sub_t = lax.broadcasted_iota(jnp.int32, (chunk, nodes), 0)
    lane_t = lax.broadcasted_iota(jnp.int32, (chunk, nodes), 1) * degree
    tall = (sub_t >= lane_t) & (sub_t < lane_t + degree)
    out = dict(tall=to_bf(tall), wide=to_bf(wide), sum=jnp.where(wide, mask_rows[:1], 0.0).astype(BF))
    if mask_col is not None:
        out['spread'] = jnp.where(tall, jnp.concatenate([mask_col] * (nodes // LANES), axis=1), 0.0).astype(BF)
    return out


def make_tables(tiles, slots, tile_nodes, send_ids, mask_ref, node_ref, gcol_ref, grow_ref, nrow_ref, mcol_ref, mrow_ref, pack_ref, out_ref):
    me = lax.axis_index('sp')
    ids = send_ids[...]
    edges = ids.shape[1]
    tile_of = ids // tile_nodes
    local = (ids - tile_of * tile_nodes).astype(F32)
    row = lax.broadcasted_iota(jnp.int32, (tiles, edges), 0)
    is_me = row == me
    own_tile = jnp.sum(jnp.where(is_me, tile_of, 0), axis=0, keepdims=True)
    own_local = jnp.sum(jnp.where(is_me, local, 0.0), axis=0, keepdims=True)
    own = jnp.where(own_tile == row, 1.0, 0.0)
    inc = jnp.where((tile_of == me) & jnp.logical_not(is_me), 1.0, 0.0)
    both = jnp.concatenate([own, inc], axis=0).astype(BF)
    rank = jnp.zeros((2 * tiles, edges), F32)
    step = 256
    for blk in range(edges // step):
        first = lax.broadcasted_iota(jnp.int32, (step, edges), 0) + blk * step
        second = lax.broadcasted_iota(jnp.int32, (step, edges), 1)
        rank += dot_nn(both[:, blk * step:(blk + 1) * step], to_bf(first < second))
    slot_id = jnp.where(is_me, own_local, rank[:tiles] + (row * slots + tile_nodes).astype(F32))
    gidx = jnp.sum(own * slot_id, axis=0, keepdims=True)
    grow_ref[...] = jnp.broadcast_to(gidx, grow_ref.shape).astype(jnp.int32)
    gcol_ref[...] = jnp.transpose(jnp.broadcast_to(gidx, (LANES, edges))).astype(jnp.int32)
    mask = mask_ref[...].astype(F32)
    mrow_ref[...] = jnp.broadcast_to(mask, mrow_ref.shape)
    mcol_ref[...] = jnp.transpose(jnp.broadcast_to(mask, (LANES, edges)))
    slot_row = lax.broadcasted_iota(jnp.int32, (slots, edges), 0).astype(F32)
    cols = []
    for peer in range(tiles):
        hit = (slot_row == rank[tiles + peer:tiles + peer + 1]) & (inc[peer:peer + 1] > 0.5)
        found = jnp.sum(jnp.where(hit, local[peer:peer + 1] + 1.0, 0.0), axis=1, keepdims=True) - 1.0
        cols.append(jnp.broadcast_to(found, (slots, LANES)))
    ncol_f = jnp.concatenate(cols, axis=0)
    ncol = ncol_f.astype(jnp.int32)
    nrow_ref[...] = jnp.transpose(ncol_f)[:8].astype(jnp.int32)
    group = 4
    for part in range(tiles // group):
        rows = group * slots
        pick = onehot_cols(ncol[part * rows:(part + 1) * rows], 0, tile_nodes)
        pack_ref[part * rows:(part + 1) * rows, :] = pick
        for sample in range(out_ref.shape[1]):
            got = dot_nn(pick, node_ref[sample]).astype(BF)
            out_ref[part * group:(part + 1) * group, sample] = got.reshape(group, slots, got.shape[1])


def fill_rows(rows_ref, node, got, tile_nodes):
    rows_ref[:tile_nodes, :] = node
    rows_ref[tile_nodes:, :] = got.reshape(got.shape[0] * got.shape[1], got.shape[2])


def build_pick(gcol_ref, pick_ref):
    step = 128 * 3

    def build(i, carry):
        base = pl.multiple_of(i * step, step)
        pick_ref[pl.ds(base, step), :] = onehot_cols(gcol_ref[pl.ds(base, step), :], 0, pick_ref.shape[1])
        return carry
    lax.fori_loop(0, pick_ref.shape[0] // step, build, 0)


def fwd_sample(maps, v_c, e_c, pick_ref, rows_ref, wts, norm_ref):
    w_e1, w_e2, w_n1, w_n2 = wts
    width = e_c.shape[-1]
    w_edge, w_send, w_recv = (w_e1[i * width:(i + 1) * width, :] for i in range(w_e1.shape[0] // width))
    sent = dot_nn(pick_ref[...], rows_ref[...]).astype(BF)
    recv = dot_nn(maps['tall'], v_c).astype(BF)
    pre = dot_nn(e_c, w_edge) + dot_nn(sent, w_send) + dot_nn(recv, w_recv)
    rows = [norm_ref[i:i + 1, :] for i in range(len(SHARD_ROWS))]
    branch, edge_s = branch_forward(pre, w_e2[...], rows[0], rows[1])
    e_new = (e_c.astype(F32) + branch).astype(BF)
    sums = dot_nn(maps['sum'], e_new).astype(BF)
    pre_n = dot_nn(v_c, w_n1[:width, :]) + dot_nn(sums, w_n1[width:, :])
    branch_n, node_s = branch_forward(pre_n, w_n2[...], rows[2], rows[3])
    return e_new, sums, branch_n, edge_s, node_s


def ids_kernel(tiles, slots, tile_nodes, mine_ref, ids_ref, most_ref, wide, send_sem, recv_sem):
    me = lax.axis_index('sp')
    peers = tile_peers(tiles)
    greet(peers)
    wide[me] = mine_ref[...]
    greeted(len(peers))
    copies = [pltpu.make_async_remote_copy(src_ref=mine_ref, dst_ref=wide.at[me], send_sem=send_sem.at[spot], recv_sem=recv_sem.at[spot], device_id=peer, device_id_type=MESH_ID) for spot, peer in enumerate(peers)]
    for copy in copies:
        copy.start()
    for copy in copies:
        copy.wait()
    for line in range(wide.shape[1]):
        ids_ref[:, line * LANES:(line + 1) * LANES] = wide[:, line, :]
    tile_of = ids_ref[...] // tile_nodes
    row = lax.broadcasted_iota(jnp.int32, (tiles, LANES), 0)
    most = jnp.zeros((tiles, LANES), F32)
    for peer in range(tiles):
        count = jnp.sum(jnp.where(tile_of == peer, 1.0, 0.0), axis=1, keepdims=True)
        most = jnp.maximum(most, jnp.where(row == peer, 0.0, count))
    most_ref[...] = jnp.broadcast_to(jnp.max(most, axis=0, keepdims=True), most_ref.shape)


def open_kernel(cfg, shards, send_ids, mask_ref, nodes_ref, node_ref, edge_ref, dnode_ref, dedge_ref, m_e1, m_e2, m_n1, m_n2, m_norm,
                vout_ref, he_ref, ye_ref, sum_ref, hn_ref, yn_ref, de_ref, dloc_ref, sloc_ref, grad_ref, grow_ref, nrow_ref, mcol_ref, mrow_ref, w_e1, w_e2, w_n1, w_n2, norm_ref, recv_out,
                gcol_ref, pick_ref, drop_ref, pack_ref, rows_ref, dpre_ref, e_two, v_two, out_buf, in_buf, next_buf, in_two, part_ref, gat_ref,
                send_a, recv_a, self_a, send_b, recv_b, self_b, send_c, recv_c, self_c, send_w, recv_w, self_w, send_x, recv_x, self_x):
    tiles, slots, tile_nodes, degree = cfg
    samples = nodes_ref.shape[0]
    all_wts = (w_e1, w_e2, w_n1, w_n2)
    step = pl.program_id(0)
    weight_sems = ((send_w, recv_w, self_w), (send_x, recv_x, self_x))

    def take_weights(layer):
        shards_wait(part_ref.at[layer], gat_ref.at[layer], *weight_sems[layer], shards, False)
        load_weights(gat_ref.at[layer], layer, all_wts, norm_ref)

    @pl.when(step == 0)
    def _():
        peers = tile_peers(tiles) + shard_peers(shards)
        greet(peers)
        cast_parts((m_e1, m_e2, m_n1, m_n2, m_norm), part_ref)
        make_tables(tiles, slots, tile_nodes, send_ids, mask_ref, nodes_ref, gcol_ref, grow_ref, nrow_ref, mcol_ref, mrow_ref, pack_ref, out_buf)
        greeted(len(peers))
        for sample in range(samples):
            slots_start(out_buf, in_buf, sample, send_a, recv_a, self_a, tiles)
        for layer, sems in enumerate(weight_sems):
            shards_start(part_ref.at[layer], gat_ref.at[layer], *sems, shards, False)
        build_pick(gcol_ref, pick_ref)
        take_weights(0)

    @pl.when(step < samples)
    def _():
        slots_wait(out_buf, in_buf, step, send_a, recv_a, self_a, tiles)
        fill_rows(rows_ref, node_ref[0], in_buf[:, step], tile_nodes)
        node, edge = node_ref[0], edge_ref[0]
        e_new, sums, branch_n, edge_s, node_s = fwd_sample(chunk_maps(degree, mrow_ref[...], None), node, edge, pick_ref, rows_ref, [ref.at[0] for ref in all_wts], norm_ref.at[0])
        v_new = (node.astype(F32) + branch_n).astype(BF)
        for ref, value in ((he_ref, edge_s[0]), (ye_ref, edge_s[-1]), (sum_ref, sums), (hn_ref, node_s[0]), (yn_ref, node_s[-1]), (vout_ref, v_new)):
            ref[0] = value
        e_two[step] = e_new
        v_two[step] = v_new

        def pack(i, carry):
            rows = 4 * slots
            base = pl.multiple_of(i * rows, rows)
            got = dot_nn(pack_ref[pl.ds(base, rows), :], vout_ref[0]).astype(BF)
            next_buf[pl.ds(i * 4, 4), step] = got.reshape(4, slots, got.shape[1])
            return carry
        lax.fori_loop(0, tiles // 4, pack, 0)
        slots_start(next_buf, in_two, step, send_b, recv_b, self_b, tiles)

    @pl.when(step == samples)
    def _():
        take_weights(1)
        build_drop(grow_ref, drop_ref)
        grad_ref[...] = jnp.zeros_like(grad_ref)

    @pl.when(step >= samples)
    def _():
        sample = step - samples
        slots_wait(next_buf, in_two, sample, send_b, recv_b, self_b, tiles)
        node, edge = v_two[sample], e_two[sample]
        fill_rows(rows_ref, node, in_two[:, sample], tile_nodes)
        wts, norm = [ref.at[1] for ref in all_wts], norm_ref.at[1]
        maps = chunk_maps(degree, mrow_ref[...], mcol_ref[...])
        e_new, sums, branch_n, edge_s, node_s = fwd_sample(maps, node, edge, pick_ref, rows_ref, wts, norm)
        back_sample(maps, node, edge, sums, edge_s[:-1], node_s[:-1], dnode_ref[0].astype(F32), dedge_ref, wts, norm, grad_ref, dpre_ref, de_ref, dloc_ref)
        back_pack(dpre_ref, drop_ref, sloc_ref, out_buf, sample, tiles, slots, tile_nodes)
        slots_start(out_buf, recv_out, sample, send_c, recv_c, self_c, tiles)

    @pl.when(step == 2 * samples - 1)
    def _():
        slots_wait_all(out_buf, recv_out, samples, send_c, recv_c, self_c, tiles)


def back_sample(maps, v_c, e_c, sums, edge_s, node_s, d_node, dedge_ref, wts, norm_ref, grad_ref, dpre_ref, de_ref, dloc_ref):
    w_e1, w_e2, w_n1, w_n2 = wts
    width = e_c.shape[-1]
    w_edge, w_send, w_recv = (w_e1[i * width:(i + 1) * width, :] for i in range(w_e1.shape[0] // width))
    d_pre_n, d_wn2, d_gain_n, d_bias_n = branch_backward(d_node, *node_s, w_n2[...], norm_ref[2:3, :])
    d_in_v = dot_nt(d_pre_n, w_n1[:width, :])
    d_sum = dot_nt(d_pre_n, w_n1[width:, :]).astype(BF)
    d_res = (dedge_ref[0].astype(F32) + dot_nn(maps['spread'], d_sum)).astype(BF).astype(F32)
    d_pre, d_we2, d_gain_e, d_bias_e = branch_backward(d_res, *edge_s, w_e2[...], norm_ref[0:1, :])
    dpre_ref[...] = d_pre
    de_ref[0] = (d_res + dot_nt(d_pre, w_edge)).astype(BF)
    recv = split_three(dot_nn(maps['wide'], d_pre))
    dloc_ref[0] = d_node + d_in_v + sum(dot_nt(piece, w_recv) for piece in recv)
    blocks = [dot_tn(e_c, d_pre), None, sum(dot_tn(v_c, piece) for piece in recv), d_we2, dot_tn(v_c, d_pre_n), dot_tn(sums, d_pre_n), d_wn2]
    for i, block in enumerate(blocks):
        if block is not None:
            grad_ref[i * width:(i + 1) * width, :] += block
    rows = [d_gain_e, d_bias_e, d_gain_n, d_bias_n]
    grad_ref[len(blocks) * width:, :] += jnp.concatenate(rows + [jnp.zeros((len(rows), width), F32)], axis=0)


def back_pack(dpre_ref, drop_ref, sloc_ref, send_buf, step, tiles, slots, tile_nodes):
    sloc_ref[0] = dot_nn(drop_ref[:tile_nodes, :], dpre_ref[...])

    def pack(i, carry):
        rows = 4 * slots
        base = pl.multiple_of(tile_nodes + i * rows, 64)
        got = dot_nn(drop_ref[pl.ds(base, rows), :], dpre_ref[...]).astype(BF)
        send_buf[pl.ds(i * 4, 4), step] = got.reshape(4, slots, got.shape[1])
        return carry
    lax.fori_loop(0, tiles // 4, pack, 0)


def build_drop(grow_ref, drop_ref):
    step = 256

    def build(i, carry):
        base = pl.multiple_of(i * step, step)
        drop_ref[pl.ds(base, step), :] = onehot_rows(grow_ref[0:1, :], base, step)
        return carry
    lax.fori_loop(0, drop_ref.shape[0] // step, build, 0)


def again(pre_b, out_b):
    pre_f = pre_b.astype(F32)
    sig = jax.nn.sigmoid(pre_f)
    act = (pre_f * sig).astype(BF)
    normed, inv_std = norm_parts(out_b)
    return pre_b, act, sig, normed, inv_std


def backward_kernel(cfg, shards, node_ref, edge_ref, he_ref, ye_ref, sum_ref, hn_ref, yn_ref, dedge_ref, grow_ref, mrow_ref, mcol_ref, nrow_ref, w_e1, w_e2, w_n1, w_n2, norms_ref, vall_ref, dlall_ref, slall_ref, recv_ref, gtwo_ref,
                    de_ref, dloc_ref, sloc_ref, grad_ref, recv_out, part_out,
                    drop_ref, dpre_ref, fold_ref, gsend_ref, dv_ref, full_ref, send_buf, send_b, recv_b, self_b, send_w, recv_w, self_w):
    tiles, slots, tile_nodes, degree = cfg
    samples = vall_ref.shape[0]
    step = pl.program_id(0)

    @pl.when(step == 0)
    def _():
        peers = tile_peers(tiles) + shard_peers(shards)
        greet(peers)
        fold_ref[...] = onehot_rows(nrow_ref[:1], 0, tile_nodes)
        gsend_ref[...] = jnp.zeros_like(gsend_ref)

        def finish(sample, carry):
            dv_ref[sample] = finish_sample(vall_ref[sample], dlall_ref[sample], slall_ref[sample], recv_ref[:, sample], fold_ref, gsend_ref, w_e1.at[1])
            return carry
        lax.fori_loop(0, samples, finish, 0)
        lay_grads(full_ref, gtwo_ref, gsend_ref)
        greeted(len(peers))
        shards_start(full_ref, part_out, send_w, recv_w, self_w, shards, True)
        build_drop(grow_ref, drop_ref)
        grad_ref[...] = jnp.zeros_like(grad_ref)

    maps = chunk_maps(degree, mrow_ref[...], mcol_ref[...])
    edge_s = again(he_ref[0], ye_ref[0])
    node_s = again(hn_ref[0], yn_ref[0])
    back_sample(maps, node_ref[0], edge_ref[0], sum_ref[0], edge_s, node_s, dv_ref[step].astype(F32), dedge_ref, [ref.at[0] for ref in (w_e1, w_e2, w_n1, w_n2)], norms_ref.at[0], grad_ref, dpre_ref, de_ref, dloc_ref)
    back_pack(dpre_ref, drop_ref, sloc_ref, send_buf, step, tiles, slots, tile_nodes)
    slots_start(send_buf, recv_out, step, send_b, recv_b, self_b, tiles)

    @pl.when(step == samples - 1)
    def _():
        shards_wait(full_ref, part_out, send_w, recv_w, self_w, shards, True)
        slots_wait_all(send_buf, recv_out, samples, send_b, recv_b, self_b, tiles)


def finish_sample(node, d_loc, s_loc, got, fold_ref, gsend_ref, w_e1):
    width = node.shape[-1]
    total = s_loc + dot_nn(fold_ref[...], got.reshape(got.shape[0] * got.shape[1], width))
    pieces = split_three(total)
    w_send = w_e1[width:2 * width, :]
    gsend_ref[...] += sum(dot_tn(node, piece) for piece in pieces)
    return (d_loc + sum(dot_nt(piece, w_send) for piece in pieces)).astype(BF)


def lay_grads(full_ref, grad_ref, gsend_ref):
    shards, rows_all, width = full_ref.shape
    sources = ((grad_ref, 0), (gsend_ref, 0), (grad_ref, 2 * width))
    for shard in range(shards):
        row = SHARD_ROWS[0] * shard
        last = row + SHARD_ROWS[0]
        spot = 0
        while row < last:
            block = row // width
            count = min(last, (block + 1) * width) - row
            ref, base = sources[block]
            base = base + row - block * width
            full_ref[shard, spot:spot + count, :] = ref[base:base + count, :]
            row += count
            spot += count
        first = 3 * width
        for rows, off in zip(SHARD_ROWS[1:], SHARD_OFF[1:]):
            full_ref[shard, off:off + rows, :] = grad_ref[first + shard * rows:first + (shard + 1) * rows, :]
            first += rows * shards
        full_ref[shard, NORM_OFF:NORM_OFF + 8, :] = grad_ref[first:first + 8, :]
        full_ref[shard, NORM_OFF + 8:, :] = jnp.zeros((rows_all - NORM_OFF - 8, width), F32)


def finish_kernel(cfg, samples, node_ref, dloc_ref, sloc_ref, recv_ref, de_ref, nrow_ref, w_e1, grad_ref, dv_ref, dout_ref, full_ref, fold_ref, gsend_ref):
    tile_nodes = node_ref.shape[1]
    step = pl.program_id(0)

    @pl.when(step == 0)
    def _():
        fold_ref[...] = onehot_rows(nrow_ref[:1], 0, tile_nodes)
        gsend_ref[...] = jnp.zeros_like(gsend_ref)

    dv_ref[0] = finish_sample(node_ref[0], dloc_ref[0], sloc_ref[0], recv_ref[:, 0], fold_ref, gsend_ref, w_e1.at[0])
    dout_ref[0] = de_ref[0]

    @pl.when(step == samples - 1)
    def _():
        lay_grads(full_ref, grad_ref, gsend_ref)


def adam_kernel(shards, both_ref, *refs):
    dp = lax.axis_index('dp')
    masters, ones, twos, new_masters, new_ones, new_twos = (refs[i:i + 5] for i in range(0, len(refs), 5))
    layers, gains, lanes = masters[-1].shape
    norm = both_ref[:, NORM_OFF:NORM_OFF + gains, :lanes]
    for shard in range(1, shards):
        norm = jnp.where(dp == shard, both_ref[:, NORM_OFF:NORM_OFF + gains, shard * lanes:(shard + 1) * lanes], norm)
    sums = [both_ref[:, off:off + rows, :] for rows, off in zip(SHARD_ROWS, SHARD_OFF)] + [norm]
    for slot, grad_sum in enumerate(sums):
        results = adamw_update(masters[slot][...], grad_sum, ones[slot][...], twos[slot][...])
        for ref, value in zip((new_masters[slot], new_ones[slot], new_twos[slot]), results):
            ref[...] = value


def tail_kernel(tiles, shards, full_ref, part_ref, out_ref, half_buf, x_buf, own, rs_buf, piece, gath, s0, r0, s1, r1, s2, r2, s3, r3):
    me = lax.axis_index('sp')
    dp = lax.axis_index('dp')
    core = lax.rem(dp, 2)
    chip = dp // 2
    chips = shards // 2
    partner = (me, dp + 1 - 2 * core)
    away = line_first(chips)
    spots = [lax.rem(chip + offset, chips) for offset in away]
    line = [(me, spot * 2 + core) for spot in spots]
    plane = tile_peers(tiles)
    greet([partner] + line + plane)
    greeted(1 + len(line) + len(plane))

    pair = [pltpu.make_async_remote_copy(src_ref=full_ref.at[spot * 2 + 1 - core], dst_ref=half_buf.at[spot], send_sem=s0.at[k], recv_sem=r0.at[k], device_id=partner, device_id_type=MESH_ID) for k, spot in enumerate(spots + [chip])]
    for copy in pair:
        copy.start()
    total = part_ref[0]
    for shard in range(1, shards):
        total += part_ref[shard]
    own[1] = total
    hops = []
    for k, spot in enumerate(spots):
        pair[k].wait()
        half_buf[spot] += full_ref[spot * 2 + core]
        hop = pltpu.make_async_remote_copy(src_ref=half_buf.at[spot], dst_ref=x_buf.at[chip], send_sem=s1.at[k], recv_sem=r1.at[k], device_id=line[k], device_id_type=MESH_ID)
        hop.start()
        hops.append(hop)
    pair[-1].wait()
    total = half_buf[chip] + full_ref[dp]
    for hop, offset in zip(hops, away):
        hop.wait()
        total += x_buf[lax.rem(chip + chips - offset, chips)]
    own[0] = total

    rows = FULL_ROWS // tiles
    cuts = []
    for k, peer in enumerate(plane):
        cut = pltpu.make_async_remote_copy(src_ref=own.at[:, pl.ds(pl.multiple_of(peer[0] * rows, rows), rows)], dst_ref=rs_buf.at[me], send_sem=s2.at[k], recv_sem=r2.at[k], device_id=peer, device_id_type=MESH_ID)
        cut.start()
        cuts.append(cut)
    here = pl.ds(pl.multiple_of(me * rows, rows), rows)
    for cut in cuts:
        cut.wait()
    total = own[:, here, :]
    for offset in range(1, tiles):
        total += rs_buf[lax.rem(me + offset, tiles)]
    piece[...] = total
    gath[:, here, :] = total
    sends = []
    for k, peer in enumerate(plane):
        send = pltpu.make_async_remote_copy(src_ref=piece, dst_ref=gath.at[:, here], send_sem=s3.at[k], recv_sem=r3.at[k], device_id=peer, device_id_type=MESH_ID)
        send.start()
        sends.append(send)
    for send in sends:
        send.wait()
    out_ref[...] = gath[...]


def whole(shape):
    zeros = (0,) * len(shape)
    return pl.BlockSpec(shape, lambda s: zeros)


def per_sample(rows, width):
    return pl.BlockSpec((1, rows, width), lambda s: (s, 0, 0))


def slot_spec(tiles, slots, width):
    return pl.BlockSpec((tiles, 1, slots, width), lambda s: (0, s, 0, 0))


PARAMS = dict(vmem_limit_bytes=63 << 20)


def grid_params():
    return pltpu.CompilerParams(dimension_semantics=("arbitrary",), **PARAMS)


def remote_params(number):
    return pltpu.CompilerParams(collective_id=number, has_side_effects=True, **PARAMS)


def slot_sems(samples, tiles):
    return [pltpu.SemaphoreType.DMA((samples, tiles)), pltpu.SemaphoreType.DMA((samples, tiles)), pltpu.SemaphoreType.DMA((samples,))]


def shard_sems(shards):
    return [pltpu.SemaphoreType.DMA((shards,)), pltpu.SemaphoreType.DMA((shards,)), pltpu.SemaphoreType.DMA]


def solution(mesh):
    lat_spec = P('dp', 'sp', None)
    edge_spec = P('sp')
    mat_spec = P(None, 'dp', None)
    norm_spec = P(None, None, 'dp')
    param_specs = (mat_spec, mat_spec, mat_spec, mat_spec, norm_spec)
    tiles = mesh.shape['sp']
    dp_size = mesh.shape['dp']

    def spread(value, axis):
        count = mesh.shape[axis]
        return lax.all_to_all(jnp.broadcast_to(value[None], (count,) + value.shape), axis, 0, 0, tiled=True)

    def join(stacked, dim):
        moved = jnp.moveaxis(stacked, 0, dim)
        return moved.reshape(moved.shape[:dim] + (moved.shape[dim] * moved.shape[dim + 1],) + moved.shape[dim + 2:])

    def scatter_sum(value, axis, dim):
        count = mesh.shape[axis]
        split = value.reshape(value.shape[:dim] + (count, value.shape[dim] // count) + value.shape[dim + 1:])
        return jnp.sum(lax.all_to_all(jnp.moveaxis(split, dim, 0), axis, 0, 0, tiled=True), axis=0)

    def gather_weights(masters, layer_idx):
        mat_list = [join(spread(master[layer_idx].astype(BF), 'dp'), 0) for master in masters[:4]]
        norm_rows = join(spread(masters[4][layer_idx].astype(BF), 'dp'), 1).astype(F32)
        return mat_list[0], mat_list[1], mat_list[2], mat_list[3], norm_rows

    def reduce_grads(grads):
        parts = [scatter_sum(grad_full, 'dp', 0) for grad_full in grads[:4]] + [scatter_sum(grads[4], 'dp', 1)]
        return tuple(jnp.sum(spread(part, 'sp'), axis=0) for part in parts)

    def general_step(node_lat, edge_lat, senders, edge_mask, node_cot, edge_cot, masters):
        batch_size, tile_nodes, lat_width = node_lat.shape
        degree = edge_lat.shape[1] // tile_nodes
        layers = masters[0].shape[0]
        mask_f = edge_mask.astype(F32).reshape(tile_nodes, degree)
        mask_b = mask_f.astype(BF)
        node_x = node_lat
        edge_x = edge_lat.reshape(batch_size, tile_nodes, degree, lat_width)
        records = []
        for layer_idx in range(layers):
            layer_wts = gather_weights(masters, layer_idx)
            node_all = join(spread(node_x, 'sp'), 1)
            node_new, edge_new, saved = layer_forward(node_x, node_all, edge_x, senders, mask_b, layer_wts)
            records.append((node_x, edge_x, saved))
            node_x = node_new
            edge_x = edge_new
        d_node = node_cot
        d_edge = edge_cot.reshape(batch_size, tile_nodes, degree, lat_width)
        grads_rev = []
        for layer_idx in reversed(range(layers)):
            layer_wts = gather_weights(masters, layer_idx)
            node_in, edge_in, saved = records[layer_idx]
            d_local, scattered, d_edge, grads = layer_backward(d_node, d_edge, node_in, edge_in, senders, mask_f, saved, layer_wts, tile_nodes * tiles)
            returned = scatter_sum(scattered, 'sp', 1)
            d_node = (d_local + returned).astype(BF)
            grads_rev.append(reduce_grads(grads))
        layer_grads = grads_rev[::-1]
        sums = tuple(jnp.stack([per_layer[slot] for per_layer in layer_grads], axis=0) for slot in range(5))
        return sums + (d_node, d_edge.reshape(edge_lat.shape))

    def compact_step(node_lat, edge_lat, send_all, edge_mask, node_cot, edge_cot, masters):
        samples, tile_nodes, width = node_lat.shape
        edges = edge_lat.shape[1]
        cfg = (tiles, SLOTS, tile_nodes, edges // tile_nodes)
        cols = tile_nodes + tiles * SLOTS
        layers = masters[0].shape[0]
        sd = jax.ShapeDtypeStruct
        vmem = pl.BlockSpec(memory_space=pltpu.VMEM)
        hbm = pl.BlockSpec(memory_space=pl.ANY)
        last = samples - 1

        def early(rows):
            return pl.BlockSpec((1, rows, width), lambda s: (jnp.minimum(s, last), 0, 0))

        def late(rows):
            return pl.BlockSpec((1, rows, width), lambda s: (jnp.maximum(s - samples, 0), 0, 0))

        node_b = sd((samples, tile_nodes, width), BF)
        node_f = sd((samples, tile_nodes, width), F32)
        edge_b = sd((samples, edges, width), BF)
        grad_f = sd((GRAD_ROWS, width), F32)
        slot_b = sd((tiles, samples, SLOTS, width), BF)
        full_f = sd((dp_size, FULL_ROWS, width), F32)
        grow_b = sd((8, edges), jnp.int32)
        nrow_b = sd((8, tiles * SLOTS), jnp.int32)
        mcol_b = sd((edges, LANES), F32)
        mrow_b = sd((8, edges), F32)
        weights_b = [sd((layers, rows * dp_size, width), BF) for rows in SHARD_ROWS] + [sd((layers, 8, width), F32)]

        def full_specs(shapes):
            return [whole(item.shape) for item in shapes]

        def scratch(shape, kind=BF):
            return pltpu.VMEM(shape, kind)

        slot_v = scratch(slot_b.shape)
        drop_v = scratch((cols, edges))
        dpre_v = scratch((edges, width))
        fold_v = scratch((tile_nodes, tiles * SLOTS))
        gsend_v = scratch((width, width), F32)
        tables_b = [grow_b, nrow_b, mcol_b, mrow_b]
        outs = pl.pallas_call(
            functools.partial(open_kernel, cfg, dp_size), grid=(2 * samples,),
            out_shape=[node_b, edge_b, edge_b, node_b, node_b, node_b, edge_b, node_f, node_f, grad_f] + tables_b + weights_b + [slot_b],
            in_specs=[whole((tiles, edges)), whole((1, edges)), whole(node_b.shape), early(tile_nodes), early(edges), late(tile_nodes), late(edges)] + [whole(master.shape) for master in masters],
            out_specs=[early(tile_nodes), early(edges), early(edges), early(tile_nodes), early(tile_nodes), early(tile_nodes), late(edges), late(tile_nodes), late(tile_nodes)] + full_specs([grad_f] + tables_b + weights_b) + [hbm],
            scratch_shapes=[scratch(mcol_b.shape, jnp.int32), scratch((edges, cols)), drop_v, scratch((tiles * SLOTS, tile_nodes)), scratch((cols, width)), dpre_v, scratch(edge_b.shape), scratch(node_b.shape),
                            slot_v, slot_v, slot_v, slot_v, scratch((layers, PART_ROWS, width)), scratch((layers, dp_size, PART_ROWS, width))]
            + slot_sems(samples, tiles) + slot_sems(samples, tiles) + slot_sems(samples, tiles) + shard_sems(dp_size) + shard_sems(dp_size),
            name='open', compiler_params=remote_params(1))(send_all, edge_mask.reshape(1, edges), node_lat, node_lat, edge_lat, node_cot, edge_cot, *masters)
        v_one, h_e, y_e, sums, h_n, y_n, d_edge, d_loc, s_loc, grad_two, grow, nrow, mcol, mrow = outs[:14]
        weights = outs[14:-1]
        recv_three = outs[-1]

        node_s = per_sample(tile_nodes, width)
        edge_s = per_sample(edges, width)
        d_edge0, d_loc0, s_loc0, grad_one, recv_four, part_two = pl.pallas_call(
            functools.partial(backward_kernel, cfg, dp_size), grid=(samples,),
            out_shape=(edge_b, node_f, node_f, grad_f, slot_b, full_f),
            in_specs=[node_s, edge_s, edge_s, edge_s, node_s, node_s, node_s, edge_s] + full_specs([grow_b, mrow_b, mcol_b, nrow_b] + weights_b + [node_b, node_f, node_f, slot_b, grad_f]),
            out_specs=[edge_s, node_s, node_s, whole(grad_f.shape), hbm, hbm],
            scratch_shapes=[drop_v, dpre_v, fold_v, gsend_v, scratch(node_b.shape), scratch(full_f.shape, F32), slot_v] + slot_sems(samples, tiles) + shard_sems(dp_size),
            name='backward_one', compiler_params=remote_params(2))(node_lat, edge_lat, h_e, y_e, sums, h_n, y_n, d_edge, grow, mrow, mcol, nrow, *weights, v_one, d_loc, s_loc, recv_three, grad_two)

        d_node, d_edge, full_one = pl.pallas_call(
            functools.partial(finish_kernel, cfg, samples), grid=(samples,),
            out_shape=(node_b, edge_b, full_f),
            in_specs=[node_s, node_s, node_s, slot_spec(tiles, SLOTS, width), edge_s] + full_specs([nrow_b, weights_b[0], grad_f]),
            out_specs=[node_s, edge_s, whole(full_f.shape)],
            scratch_shapes=[fold_v, gsend_v],
            name='finish', compiler_params=grid_params())(node_lat, d_loc0, s_loc0, recv_four, d_edge0, nrow, weights[0], grad_one)

        rows = FULL_ROWS // tiles
        few = pltpu.SemaphoreType.DMA((tiles,))
        both_f = (layers, FULL_ROWS, width)
        half_v = scratch((dp_size // 2, FULL_ROWS, width), F32)
        both = pl.pallas_call(
            functools.partial(tail_kernel, tiles, dp_size),
            out_shape=sd(both_f, F32), in_specs=[vmem, vmem], out_specs=vmem,
            scratch_shapes=[half_v, half_v, scratch(both_f, F32), scratch((tiles, layers, rows, width), F32), scratch((layers, rows, width), F32), scratch(both_f, F32)] + [few] * 8,
            name='tail', compiler_params=remote_params(3))(full_one, part_two)
        return both, d_node, d_edge

    def general_both(*args):
        result = general_step(*args)
        lanes = result[4].shape[-1]
        first = result[0]
        norm = lax.dynamic_update_slice(jnp.zeros((first.shape[0], FULL_ROWS - NORM_OFF, first.shape[-1]), F32), result[4], (0, 0, lax.axis_index('dp') * lanes))
        return jnp.concatenate(result[:4] + (norm,), axis=1), result[5], result[6]

    def train_step(node_lat, edge_lat, senders, edge_mask, node_cot, edge_cot, w_edge1, w_edge2, w_node1, w_node2, norm_par, mom_edge1, mom_edge2, mom_node1, mom_node2, mom_norm, vel_edge1, vel_edge2, vel_node1, vel_node2, vel_norm):
        masters = (w_edge1, w_edge2, w_node1, w_node2, norm_par)
        moments_one = (mom_edge1, mom_edge2, mom_node1, mom_node2, mom_norm)
        moments_two = (vel_edge1, vel_edge2, vel_node1, vel_node2, vel_norm)
        tile_nodes = node_lat.shape[1]
        lines = senders.shape[0] // LANES
        vmem = pl.BlockSpec(memory_space=pltpu.VMEM)
        few = pltpu.SemaphoreType.DMA((tiles,))
        send_all, most = pl.pallas_call(
            functools.partial(ids_kernel, tiles, SLOTS, tile_nodes),
            out_shape=(jax.ShapeDtypeStruct((tiles, lines * LANES), jnp.int32), jax.ShapeDtypeStruct((8, LANES), F32)),
            in_specs=[vmem], out_specs=(vmem, vmem), scratch_shapes=[pltpu.VMEM((tiles, lines, LANES), jnp.int32), few, few],
            name='ids', compiler_params=remote_params(0))(senders.reshape(lines, LANES))
        fits = most[0, 0] <= SLOTS

        def unsettled(state):
            return jnp.logical_not(state[0])

        def settle(state):
            held = tuple(master * jnp.logical_not(state[0]).astype(F32) for master in masters)
            args = (node_lat, edge_lat, senders, edge_mask, node_cot, edge_cot, held)
            return (True,) + jax.tree.map(row_major, general_both(*jax.tree.map(row_major, args)))

        state = (fits,) + compact_step(node_lat, edge_lat, send_all, edge_mask, node_cot, edge_cot, masters)
        both, d_node, d_edge = lax.while_loop(unsettled, settle, state)[1:]
        state = masters + moments_one + moments_two
        new_state = pl.pallas_call(
            functools.partial(adam_kernel, dp_size), out_shape=[jax.ShapeDtypeStruct(item.shape, F32) for item in state],
            in_specs=[vmem] * (len(state) + 1), out_specs=[vmem] * len(state), name='adam', compiler_params=pltpu.CompilerParams(**PARAMS))(both, *state)
        return tuple(new_state) + (d_node, d_edge)

    return jax.shard_map(train_step, mesh=mesh, in_specs=(lat_spec, lat_spec, edge_spec, edge_spec, lat_spec, lat_spec) + param_specs + param_specs + param_specs, out_specs=param_specs + param_specs + param_specs + (lat_spec, lat_spec), check_vma=False)
```

profile of v0, /device:TPU:1, one launch (start us, length us, event | category | flops | bytes accessed | tf_op | source)
XLA Modules:
  0.0 234.8 jit_solution(8099599140480622492)
XLA Ops:
  0.7 0.0 copy-start.4
  0.7 1.4 reshape.311.mask_ref
  2.0 12.1 %ids.1 = (s32[16,1536]{1,0:T(8,128)}, f32[8,128]{1,0:T(8,128)}) custom-call(s32[12,128]{1,0:T(8,128)} %bitcast.349), custom_call_target="tpu_custom_call" | custom-call | tf_op jit(solution)/shard_map/ids/pallas_call | solution.py:884
  14.1 1.2 slice.158
  16.0 114.7 %open.1 = (bf16[4,256,256]{2,1,0:T(8,128)(2,1)}, bf16[4,1536,256]{2,1,0:T(8,128)(2,1)}, bf16[4,1536,256]{2,1,0:T(8,128)(2,1)}, bf16[4,256,256]{2,1,0:T(8,128)(2,...) custom-call(s32[16,1536]{1,0:T(8,128)} %get-tuple-element.141.send_i, ...), custom_call_target="tpu_custom_call" | custom-call | tf_op jit(solution)/shard_map/open/pallas_call | solution.py:827
  130.7 0.0 copy-done.4
  130.7 51.5 %backward_one.1 = (bf16[4,1536,256]{2,1,0:T(8,128)(2,1)}, f32[4,256,256]{2,1,0:T(8,128)}, f32[4,256,256]{2,1,0:T(8,128)}, f32[1800,256]{1,0:T(8,128)}, bf16[16,4...) custom-call(bf16[4,256,256]{2,1,0:T(8,128)(2,1)S(1)} %copy-done.4, bf16[4,1536,256]{2,1,0:T(8,128)(2,1)} %edge_ref.3, ...), custom_call_target="tpu_custom_call" | custom-call | tf_op jit(solution)/shard_map/backward_one/pallas_call | solution.py:842
  182.3 0.0 copy-start.61
  182.3 0.0 copy-start.64
  182.3 0.0 copy-start.77
  182.3 0.0 copy-start.95
  182.3 9.4 %finish.1 = (bf16[4,256,256]{2,1,0:T(8,128)(2,1)}, bf16[4,1536,256]{2,1,0:T(8,128)(2,1)}, f32[8,256,256]{2,1,0:T(8,128)}) custom-call(bf16[4,256,256]{2,1,0:T(8,128)(2,1)S(1)} %copy-done.4, f32[4,256,256]{2,1,0:T(8,128)} %get-tuple-element.162.dloc_ref, f32[4,256,256]{2,1,0:T(8,128)} %get-tuple-element.163.sloc_ref, ...), custom_call_target="tpu_custom_call" | custom-call | tf_op jit(solution)/shard_map/finish/pallas_call | solution.py:850
  191.7 39.4 %tail.1 = f32[2,256,256]{2,1,0:T(8,128)} custom-call(f32[8,256,256]{2,1,0:T(8,128)} %get-tuple-element.167.full_ref, f32[8,256,256]{2,1,0:T(8,128)} %get-tuple-element.168.part_ref), custom_call_target="tpu_custom_call" | custom-call | tf_op jit(solution)/shard_map/tail/pallas_call | solution.py:862
  231.1 0.0 copy-done.61
  231.1 0.0 copy-done.64
  231.1 0.0 copy-done.77
  231.1 0.0 copy-done.95
  231.1 0.3 while.13
  231.4 3.2 %adam.1 = (f32[2,96,256]{2,1,0:T(8,128)}, f32[2,32,256]{2,1,0:T(8,128)}, f32[2,64,256]{2,1,0:T(8,128)}, f32[2,32,256]{2,1,0:T(8,128)}, f32[2,4,32]{2,1,0:T(4,128...) custom-call(f32[2,256,256]{2,1,0:T(8,128)} %get-tuple-element.468, ...), custom_call_target="tpu_custom_call" | custom-call | tf_op jit(solution)/shard_map/adam/pallas_call | solution.py:902
Async XLA Ops:
  0.7 130.1 %copy-start.4 = (bf16[4,256,256]{2,1,0:T(8,128)(2,1)S(1)}, bf16[4,256,256]{2,1,0:T(8,128)(2,1)}, u32[]{:S(2)}) copy-start(bf16[4,256,256]{2,1,0:T(8,128)(2,1)} %node_ref.5) | copy-start | bytes 1572868
  182.3 48.8 %copy-start.61 = (f32[2,96,256]{2,1,0:T(8,128)S(1)}, f32[2,96,256]{2,1,0:T(8,128)}, u32[]{:S(2)}) copy-start(f32[2,96,256]{2,1,0:T(8,128)} %refs_0_.1) | copy-start | bytes 589828
  182.3 48.8 %copy-start.64 = (f32[2,64,256]{2,1,0:T(8,128)S(1)}, f32[2,64,256]{2,1,0:T(8,128)}, u32[]{:S(2)}) copy-start(f32[2,64,256]{2,1,0:T(8,128)} %refs_2_.1) | copy-start | bytes 393220
  182.3 48.8 %copy-start.77 = (s32[1536]{0:T(1024)S(1)}, s32[1536]{0:T(1024)}, u32[]{:S(2)}) copy-start(s32[1536]{0:T(1024)} %param.27) | copy-start | bytes 18436
  182.3 48.8 %copy-start.95 = (f32[2,4,32]{2,1,0:T(4,128)S(1)}, f32[2,4,32]{2,1,0:T(4,128)}, u32[]{:S(2)}) copy-start(f32[2,4,32]{2,1,0:T(4,128)} %refs_4_.1) | copy-start | bytes 3076
where the time goes:
time: 235 us
  Pallas kernels  230 us (98%)
  local copies, waits for them, and re-layouts  2.57 us (1%)
    pallas_call x1, Pallas kernels, compact_step(): pl.pallas_call(functools.partial(open_kernel, cfg, dp_size), grid=(2 * sa...  115 us
    pallas_call x1, Pallas kernels, compact_step(): pl.pallas_call(functools.partial(backward_kernel, cfg, dp_size), grid=(sa...  51.5 us
    pallas_call x1, Pallas kernels, compact_step(): pl.pallas_call(functools.partial(tail_kernel, tiles, dp_size), out_shape=...  39.4 us
    pallas_call x1, Pallas kernels, train_step(): pl.pallas_call(functools.partial(ids_kernel, tiles, SLOTS, tile_nodes), o...  12.1 us
    pallas_call x1, Pallas kernels, compact_step(): pl.pallas_call(functools.partial(finish_kernel, cfg, samples), grid=(samp...  9.38 us

commit v1 on v0

--- a/solution.py
+++ b/solution.py
@@ -16,6 +16,8 @@
 DECAY = 0.1
 STEP = 10
 
+NODE_DIMS = (0, 1)
+EDGE_DIMS = (0, 1, 2)
 BF = jnp.bfloat16
 F32 = jnp.float32
 SLOTS = 80
@@ -103,12 +105,12 @@
     batch_size, tile_nodes, degree, lat_width = edge_x.shape
     d_res_n = d_node_new.astype(jnp.float32)
     d_pre_n, d_in_n, d_wn2, d_gain_n, d_bias_n = mlp_back(d_res_n, saved_n, w_n1, w_n2, norm_rows[2])
-    d_wn1 = jnp.concatenate([contract(node_x, d_pre_n, (0, 1), (0, 1)), contract(node_sum, d_pre_n, (0, 1), (0, 1))], axis=0)
+    d_wn1 = jnp.concatenate([contract(node_x, d_pre_n, NODE_DIMS, NODE_DIMS), contract(node_sum, d_pre_n, NODE_DIMS, NODE_DIMS)], axis=0)
     d_sum = d_in_n[..., lat_width:].astype(jnp.bfloat16)
     d_res_e = (d_edge_new.astype(jnp.float32) + d_sum.astype(jnp.float32)[:, :, None, :] * mask_f[None, :, :, None]).astype(jnp.bfloat16).astype(jnp.float32)
     d_pre_e, d_in_e, d_we2, d_gain_e, d_bias_e = mlp_back(d_res_e, saved_e, w_e1, w_e2, norm_rows[0])
-    recv_grad = contract(node_x, d_pre_e.reshape(batch_size, tile_nodes, -1), (0, 1), (0, 1))
-    d_we1 = jnp.concatenate([contract(edge_x, d_pre_e, (0, 1, 2), (0, 1, 2)), contract(sender_lat, d_pre_e, (0, 1, 2), (0, 1, 2)), recv_grad.reshape(lat_width, degree, -1).sum(axis=1)], axis=0)
+    recv_grad = contract(node_x, d_pre_e.reshape(batch_size, tile_nodes, -1), NODE_DIMS, NODE_DIMS)
+    d_we1 = jnp.concatenate([contract(edge_x, d_pre_e, EDGE_DIMS, EDGE_DIMS), contract(sender_lat, d_pre_e, EDGE_DIMS, EDGE_DIMS), recv_grad.reshape(lat_width, degree, -1).sum(axis=1)], axis=0)
     d_edge_x = (d_res_e + d_in_e[..., :lat_width]).astype(jnp.bfloat16)
     d_sender = d_in_e[..., lat_width:2 * lat_width].reshape(batch_size, tile_nodes * degree, lat_width)
     scattered = jnp.zeros((batch_size, total_nodes, lat_width), jnp.float32).at[:, senders].add(d_sender)
@@ -531,17 +533,24 @@
     return pre_b, act, sig, normed, inv_std
 
 
-def backward_kernel(cfg, shards, node_ref, edge_ref, he_ref, ye_ref, sum_ref, hn_ref, yn_ref, dedge_ref, grow_ref, mrow_ref, mcol_ref, nrow_ref, w_e1, w_e2, w_n1, w_n2, norms_ref, vall_ref, dlall_ref, slall_ref, recv_ref, gtwo_ref,
-                    de_ref, dloc_ref, sloc_ref, grad_ref, recv_out, part_out,
-                    drop_ref, dpre_ref, fold_ref, gsend_ref, dv_ref, full_ref, send_buf, send_b, recv_b, self_b, send_w, recv_w, self_w):
+def close_kernel(cfg, shards, node_ref, edge_ref, he_ref, ye_ref, sum_ref, hn_ref, yn_ref, dedge_ref, nodes_ref, grow_ref, mrow_ref, mcol_ref, nrow_ref, w_e1, w_e2, w_n1, w_n2, norms_ref, vall_ref, dlall_ref, slall_ref, recv_ref, gtwo_ref,
+                 de_ref, dv_out, both_ref,
+                 grad_ref, dloc_ref, sloc_ref, in_buf, part_buf, drop_ref, dpre_ref, fold_ref, gsend_ref, dv_ref, full_ref, send_buf, half_buf, x_buf, own, rs_buf, piece, ws_buf, gath,
+                 send_b, recv_b, self_b, send_w, recv_w, self_w, s0, r0, s1, r1, s2, r2, s3, r3, s4, r4, s5, r5, self_s):
     tiles, slots, tile_nodes, degree = cfg
     samples = vall_ref.shape[0]
     step = pl.program_id(0)
+    me = lax.axis_index('sp')
+    dp = lax.axis_index('dp')
+    core = lax.rem(dp, 2)
+    chip = dp // 2
+    chips = shards // 2
+    plane = tile_peers(tiles)
+    others = shard_peers(shards)
 
     @pl.when(step == 0)
     def _():
-        peers = tile_peers(tiles) + shard_peers(shards)
-        greet(peers)
+        greet(plane + others)
         fold_ref[...] = onehot_rows(nrow_ref[:1], 0, tile_nodes)
         gsend_ref[...] = jnp.zeros_like(gsend_ref)
 
@@ -550,22 +559,74 @@
             return carry
         lax.fori_loop(0, samples, finish, 0)
         lay_grads(full_ref, gtwo_ref, gsend_ref)
-        greeted(len(peers))
-        shards_start(full_ref, part_out, send_w, recv_w, self_w, shards, True)
+        greeted(len(plane + others))
+        shards_start(full_ref, part_buf, send_w, recv_w, self_w, shards, True)
         build_drop(grow_ref, drop_ref)
         grad_ref[...] = jnp.zeros_like(grad_ref)
 
     maps = chunk_maps(degree, mrow_ref[...], mcol_ref[...])
     edge_s = again(he_ref[0], ye_ref[0])
     node_s = again(hn_ref[0], yn_ref[0])
-    back_sample(maps, node_ref[0], edge_ref[0], sum_ref[0], edge_s, node_s, dv_ref[step].astype(F32), dedge_ref, [ref.at[0] for ref in (w_e1, w_e2, w_n1, w_n2)], norms_ref.at[0], grad_ref, dpre_ref, de_ref, dloc_ref)
-    back_pack(dpre_ref, drop_ref, sloc_ref, send_buf, step, tiles, slots, tile_nodes)
-    slots_start(send_buf, recv_out, step, send_b, recv_b, self_b, tiles)
+    back_sample(maps, node_ref[0], edge_ref[0], sum_ref[0], edge_s, node_s, dv_ref[step].astype(F32), dedge_ref, [ref.at[0] for ref in (w_e1, w_e2, w_n1, w_n2)], norms_ref.at[0], grad_ref, dpre_ref, de_ref, dloc_ref.at[pl.ds(step, 1)])
+    back_pack(dpre_ref, drop_ref, sloc_ref.at[pl.ds(step, 1)], send_buf, step, tiles, slots, tile_nodes)
+    slots_start(send_buf, in_buf, step, send_b, recv_b, self_b, tiles)
 
     @pl.when(step == samples - 1)
     def _():
-        shards_wait(full_ref, part_out, send_w, recv_w, self_w, shards, True)
-        slots_wait_all(send_buf, recv_out, samples, send_b, recv_b, self_b, tiles)
+        away = line_first(chips)
+        spots = [lax.rem(chip + offset, chips) for offset in away]
+        line = [(me, spot * 2 + core) for spot in spots]
+        shards_wait(full_ref, part_buf, send_w, recv_w, self_w, shards, True)
+        gsend_ref[...] = jnp.zeros_like(gsend_ref)
+        lay_grads(full_ref, grad_ref, gsend_ref)
+        pair = [pltpu.make_async_remote_copy(src_ref=full_ref.at[spot * 2 + 1 - core], dst_ref=half_buf.at[spot], send_sem=s0.at[k], recv_sem=r0.at[k], device_id=(me, dp + 1 - 2 * core), device_id_type=MESH_ID) for k, spot in enumerate(spots + [chip])]
+        for copy in pair:
+            copy.start()
+        own[1] = sum(part_buf[shard] for shard in range(shards))
+        hops = []
+        for k, spot in enumerate(spots):
+            pair[k].wait()
+            half_buf[spot] += full_ref[spot * 2 + core]
+            hop = pltpu.make_async_remote_copy(src_ref=half_buf.at[spot], dst_ref=x_buf.at[chip], send_sem=s1.at[k], recv_sem=r1.at[k], device_id=line[k], device_id_type=MESH_ID)
+            hop.start()
+            hops.append(hop)
+        pair[-1].wait()
+
+        def finish(sample, carry):
+            slots_wait(send_buf, in_buf, sample, send_b, recv_b, self_b, tiles)
+            dv_out[sample] = finish_sample(nodes_ref[sample], dloc_ref[sample], sloc_ref[sample], in_buf[:, sample], fold_ref, gsend_ref, w_e1.at[0])
+            return carry
+        lax.fori_loop(0, samples, finish, 0)
+        own[2] = gsend_ref[...]
+        total = half_buf[chip] + full_ref[dp]
+        for hop, offset in zip(hops, away):
+            hop.wait()
+            total += x_buf[lax.rem(chip + chips - offset, chips)]
+        own[0] = total
+
+        rows = FULL_ROWS // tiles
+        here = pl.ds(pl.multiple_of(me * rows, rows), rows)
+        cuts = [pltpu.make_async_remote_copy(src_ref=own.at[:, pl.ds(pl.multiple_of(peer[0] * rows, rows), rows)], dst_ref=rs_buf.at[me], send_sem=s2.at[k], recv_sem=r2.at[k], device_id=peer, device_id_type=MESH_ID) for k, peer in enumerate(plane)]
+        for cut in cuts:
+            cut.start()
+        for cut in cuts:
+            cut.wait()
+        piece[...] = own[:, here, :] + sum(rs_buf[lax.rem(me + offset, tiles)] for offset in range(1, tiles))
+        shards_start(piece.at[2], ws_buf, s4, r4, self_s, shards, False)
+        sends = [pltpu.make_async_remote_copy(src_ref=piece.at[:2], dst_ref=gath.at[:2, here], send_sem=s3.at[k], recv_sem=r3.at[k], device_id=peer, device_id_type=MESH_ID) for k, peer in enumerate(plane)]
+        for send in sends:
+            send.start()
+        shards_wait(piece.at[2], ws_buf, s4, r4, self_s, shards, False)
+        mine = rs_buf.at[me, 2]
+        mine[...] = sum(ws_buf[shard] for shard in range(shards))
+        more = [pltpu.make_async_remote_copy(src_ref=mine, dst_ref=gath.at[2, here], send_sem=s5.at[k], recv_sem=r5.at[k], device_id=peer, device_id_type=MESH_ID) for k, peer in enumerate(plane)]
+        for send in more:
+            send.start()
+        gath[:2, here, :] = piece[:2]
+        gath[2, here, :] = mine[...]
+        for send in sends + more:
+            send.wait()
+        both_ref[...] = gath[...]
 
 
 def finish_sample(node, d_loc, s_loc, got, fold_ref, gsend_ref, w_e1):
@@ -600,94 +661,23 @@
         full_ref[shard, NORM_OFF + 8:, :] = jnp.zeros((rows_all - NORM_OFF - 8, width), F32)
 
 
-def finish_kernel(cfg, samples, node_ref, dloc_ref, sloc_ref, recv_ref, de_ref, nrow_ref, w_e1, grad_ref, dv_ref, dout_ref, full_ref, fold_ref, gsend_ref):
-    tile_nodes = node_ref.shape[1]
-    step = pl.program_id(0)
-
-    @pl.when(step == 0)
-    def _():
-        fold_ref[...] = onehot_rows(nrow_ref[:1], 0, tile_nodes)
-        gsend_ref[...] = jnp.zeros_like(gsend_ref)
-
-    dv_ref[0] = finish_sample(node_ref[0], dloc_ref[0], sloc_ref[0], recv_ref[:, 0], fold_ref, gsend_ref, w_e1.at[0])
-    dout_ref[0] = de_ref[0]
-
-    @pl.when(step == samples - 1)
-    def _():
-        lay_grads(full_ref, grad_ref, gsend_ref)
-
-
 def adam_kernel(shards, both_ref, *refs):
+    refs, extra = refs[:-1], refs[-1]
     dp = lax.axis_index('dp')
     masters, ones, twos, new_masters, new_ones, new_twos = (refs[i:i + 5] for i in range(0, len(refs), 5))
     layers, gains, lanes = masters[-1].shape
-    norm = both_ref[:, NORM_OFF:NORM_OFF + gains, :lanes]
+    norm = both_ref[:2, NORM_OFF:NORM_OFF + gains, :lanes]
     for shard in range(1, shards):
-        norm = jnp.where(dp == shard, both_ref[:, NORM_OFF:NORM_OFF + gains, shard * lanes:(shard + 1) * lanes], norm)
-    sums = [both_ref[:, off:off + rows, :] for rows, off in zip(SHARD_ROWS, SHARD_OFF)] + [norm]
+        norm = jnp.where(dp == shard, both_ref[:2, NORM_OFF:NORM_OFF + gains, shard * lanes:(shard + 1) * lanes], norm)
+    sums = [both_ref[:2, off:off + rows, :] for rows, off in zip(SHARD_ROWS, SHARD_OFF)] + [norm]
+    rows, width = SHARD_ROWS[0], extra.shape[1]
+    extra[...] = jnp.zeros_like(extra)
+    extra[width:2 * width, :] = both_ref[2]
+    sums[0] = jnp.stack([sums[0][0] + extra[pl.ds(pl.multiple_of(dp * rows, rows), rows), :], sums[0][1]])
     for slot, grad_sum in enumerate(sums):
         results = adamw_update(masters[slot][...], grad_sum, ones[slot][...], twos[slot][...])
         for ref, value in zip((new_masters[slot], new_ones[slot], new_twos[slot]), results):
             ref[...] = value
-
-
-def tail_kernel(tiles, shards, full_ref, part_ref, out_ref, half_buf, x_buf, own, rs_buf, piece, gath, s0, r0, s1, r1, s2, r2, s3, r3):
-    me = lax.axis_index('sp')
-    dp = lax.axis_index('dp')
-    core = lax.rem(dp, 2)
-    chip = dp // 2
-    chips = shards // 2
-    partner = (me, dp + 1 - 2 * core)
-    away = line_first(chips)
-    spots = [lax.rem(chip + offset, chips) for offset in away]
-    line = [(me, spot * 2 + core) for spot in spots]
-    plane = tile_peers(tiles)
-    greet([partner] + line + plane)
-    greeted(1 + len(line) + len(plane))
-
-    pair = [pltpu.make_async_remote_copy(src_ref=full_ref.at[spot * 2 + 1 - core], dst_ref=half_buf.at[spot], send_sem=s0.at[k], recv_sem=r0.at[k], device_id=partner, device_id_type=MESH_ID) for k, spot in enumerate(spots + [chip])]
-    for copy in pair:
-        copy.start()
-    total = part_ref[0]
-    for shard in range(1, shards):
-        total += part_ref[shard]
-    own[1] = total
-    hops = []
-    for k, spot in enumerate(spots):
-        pair[k].wait()
-        half_buf[spot] += full_ref[spot * 2 + core]
-        hop = pltpu.make_async_remote_copy(src_ref=half_buf.at[spot], dst_ref=x_buf.at[chip], send_sem=s1.at[k], recv_sem=r1.at[k], device_id=line[k], device_id_type=MESH_ID)
-        hop.start()
-        hops.append(hop)
-    pair[-1].wait()
-    total = half_buf[chip] + full_ref[dp]
-    for hop, offset in zip(hops, away):
-        hop.wait()
-        total += x_buf[lax.rem(chip + chips - offset, chips)]
-    own[0] = total
-
-    rows = FULL_ROWS // tiles
-    cuts = []
-    for k, peer in enumerate(plane):
-        cut = pltpu.make_async_remote_copy(src_ref=own.at[:, pl.ds(pl.multiple_of(peer[0] * rows, rows), rows)], dst_ref=rs_buf.at[me], send_sem=s2.at[k], recv_sem=r2.at[k], device_id=peer, device_id_type=MESH_ID)
-        cut.start()
-        cuts.append(cut)
-    here = pl.ds(pl.multiple_of(me * rows, rows), rows)
-    for cut in cuts:
-        cut.wait()
-    total = own[:, here, :]
-    for offset in range(1, tiles):
-        total += rs_buf[lax.rem(me + offset, tiles)]
-    piece[...] = total
-    gath[:, here, :] = total
-    sends = []
-    for k, peer in enumerate(plane):
-        send = pltpu.make_async_remote_copy(src_ref=piece, dst_ref=gath.at[:, here], send_sem=s3.at[k], recv_sem=r3.at[k], device_id=peer, device_id_type=MESH_ID)
-        send.start()
-        sends.append(send)
-    for send in sends:
-        send.wait()
-    out_ref[...] = gath[...]
 
 
 def whole(shape):
@@ -839,39 +829,29 @@
 
         node_s = per_sample(tile_nodes, width)
         edge_s = per_sample(edges, width)
-        d_edge0, d_loc0, s_loc0, grad_one, recv_four, part_two = pl.pallas_call(
-            functools.partial(backward_kernel, cfg, dp_size), grid=(samples,),
-            out_shape=(edge_b, node_f, node_f, grad_f, slot_b, full_f),
-            in_specs=[node_s, edge_s, edge_s, edge_s, node_s, node_s, node_s, edge_s] + full_specs([grow_b, mrow_b, mcol_b, nrow_b] + weights_b + [node_b, node_f, node_f, slot_b, grad_f]),
-            out_specs=[edge_s, node_s, node_s, whole(grad_f.shape), hbm, hbm],
-            scratch_shapes=[drop_v, dpre_v, fold_v, gsend_v, scratch(node_b.shape), scratch(full_f.shape, F32), slot_v] + slot_sems(samples, tiles) + shard_sems(dp_size),
-            name='backward_one', compiler_params=remote_params(2))(node_lat, edge_lat, h_e, y_e, sums, h_n, y_n, d_edge, grow, mrow, mcol, nrow, *weights, v_one, d_loc, s_loc, recv_three, grad_two)
-
-        d_node, d_edge, full_one = pl.pallas_call(
-            functools.partial(finish_kernel, cfg, samples), grid=(samples,),
-            out_shape=(node_b, edge_b, full_f),
-            in_specs=[node_s, node_s, node_s, slot_spec(tiles, SLOTS, width), edge_s] + full_specs([nrow_b, weights_b[0], grad_f]),
-            out_specs=[node_s, edge_s, whole(full_f.shape)],
-            scratch_shapes=[fold_v, gsend_v],
-            name='finish', compiler_params=grid_params())(node_lat, d_loc0, s_loc0, recv_four, d_edge0, nrow, weights[0], grad_one)
-
         rows = FULL_ROWS // tiles
+        groups = layers + 1
+        both_f = (groups, FULL_ROWS, width)
         few = pltpu.SemaphoreType.DMA((tiles,))
-        both_f = (layers, FULL_ROWS, width)
         half_v = scratch((dp_size // 2, FULL_ROWS, width), F32)
-        both = pl.pallas_call(
-            functools.partial(tail_kernel, tiles, dp_size),
-            out_shape=sd(both_f, F32), in_specs=[vmem, vmem], out_specs=vmem,
-            scratch_shapes=[half_v, half_v, scratch(both_f, F32), scratch((tiles, layers, rows, width), F32), scratch((layers, rows, width), F32), scratch(both_f, F32)] + [few] * 8,
-            name='tail', compiler_params=remote_params(3))(full_one, part_two)
-        return both, d_node, d_edge
+        d_edge0, d_node, both = pl.pallas_call(
+            functools.partial(close_kernel, cfg, dp_size), grid=(samples,),
+            out_shape=(edge_b, node_b, sd(both_f, F32)),
+            in_specs=[node_s, edge_s, edge_s, edge_s, node_s, node_s, node_s, edge_s] + full_specs([node_b, grow_b, mrow_b, mcol_b, nrow_b] + weights_b + [node_b, node_f, node_f, slot_b, grad_f]),
+            out_specs=[edge_s] + full_specs([node_b, sd(both_f, F32)]),
+            scratch_shapes=[scratch(grad_f.shape, F32), scratch(node_f.shape, F32), scratch(node_f.shape, F32), slot_v, scratch(full_f.shape, F32), drop_v, dpre_v, fold_v, gsend_v, scratch(node_b.shape), scratch(full_f.shape, F32), slot_v,
+                            half_v, half_v, scratch(both_f, F32), scratch((tiles, groups, rows, width), F32), scratch((groups, rows, width), F32), scratch((dp_size, rows, width), F32), scratch(both_f, F32)]
+            + slot_sems(samples, tiles) + shard_sems(dp_size) + [few] * 12 + [pltpu.SemaphoreType.DMA],
+            name='close', compiler_params=remote_params(2))(node_lat, edge_lat, h_e, y_e, sums, h_n, y_n, d_edge, node_lat, grow, mrow, mcol, nrow, *weights, v_one, d_loc, s_loc, recv_three, grad_two)
+        return both, d_node, d_edge0
 
     def general_both(*args):
         result = general_step(*args)
         lanes = result[4].shape[-1]
         first = result[0]
         norm = lax.dynamic_update_slice(jnp.zeros((first.shape[0], FULL_ROWS - NORM_OFF, first.shape[-1]), F32), result[4], (0, 0, lax.axis_index('dp') * lanes))
-        return jnp.concatenate(result[:4] + (norm,), axis=1), result[5], result[6]
+        both = jnp.concatenate(result[:4] + (norm,), axis=1)
+        return jnp.concatenate([both, jnp.zeros_like(both[:1])], axis=0), result[5], result[6]
 
     def train_step(node_lat, edge_lat, senders, edge_mask, node_cot, edge_cot, w_edge1, w_edge2, w_node1, w_node2, norm_par, mom_edge1, mom_edge2, mom_node1, mom_node2, mom_norm, vel_edge1, vel_edge2, vel_node1, vel_node2, vel_norm):
         masters = (w_edge1, w_edge2, w_node1, w_node2, norm_par)
@@ -901,7 +881,7 @@
         state = masters + moments_one + moments_two
         new_state = pl.pallas_call(
             functools.partial(adam_kernel, dp_size), out_shape=[jax.ShapeDtypeStruct(item.shape, F32) for item in state],
-            in_specs=[vmem] * (len(state) + 1), out_specs=[vmem] * len(state), name='adam', compiler_params=pltpu.CompilerParams(**PARAMS))(both, *state)
+            in_specs=[vmem] * (len(state) + 1), out_specs=[vmem] * len(state), scratch_shapes=[pltpu.VMEM((w_edge2.shape[-1] * 3, w_edge2.shape[-1]), F32)], name='adam', compiler_params=pltpu.CompilerParams(**PARAMS))(both, *state)
         return tuple(new_state) + (d_node, d_edge)
 
     return jax.shard_map(train_step, mesh=mesh, in_specs=(lat_spec, lat_spec, edge_spec, edge_spec, lat_spec, lat_spec) + param_specs + param_specs + param_specs, out_specs=param_specs + param_specs + param_specs + (lat_spec, lat_spec), check_vma=False)

time: 235 us -> 221 us (0.940)
  Pallas kernels: 230 us -> 211 us
  local copies, waits for them, and re-layouts: 2.57 us -> 8.2 us
    pallas_call x3 -> x1, Pallas kernels: 100 us -> 81.5 us  [compact_step(): pl.pallas_call(functools.partial(close_kernel, cfg, dp_size), grid=(sampl...]
    unnamed x10 -> x12, local copies, waits for them, and re-layouts: 0.03 us -> 5.66 us
where the time goes in v1:
time: 221 us
  Pallas kernels  211 us (95%)
  local copies, waits for them, and re-layouts  8.2 us (4%)
    pallas_call x1, Pallas kernels, compact_step(): pl.pallas_call(functools.partial(open_kernel, cfg, dp_size), grid=(2 * sa...  114 us
    pallas_call x1, Pallas kernels, compact_step(): pl.pallas_call(functools.partial(close_kernel, cfg, dp_size), grid=(sampl...  81.5 us
    pallas_call x1, Pallas kernels, train_step(): pl.pallas_call(functools.partial(ids_kernel, tiles, SLOTS, tile_nodes), o...  12.1 us
    unnamed x12, local copies, waits for them, and re-layouts  5.66 us

profile of v1, /device:TPU:1, one launch (start us, length us, event | category | flops | bytes accessed | tf_op | source)
XLA Modules:
  0.0 221.0 jit_solution(4549252862447693972)
XLA Ops:
  0.7 0.0 copy-start.4
  0.7 1.4 reshape.311.mask_ref
  2.0 12.1 %ids.1 = (s32[16,1536]{1,0:T(8,128)}, f32[8,128]{1,0:T(8,128)}) custom-call(s32[12,128]{1,0:T(8,128)} %bitcast.349), custom_call_target="tpu_custom_call" | custom-call | tf_op jit(solution)/shard_map/ids/pallas_call | solution.py:864
  14.1 1.2 slice.158
  16.0 114.2 %open.1 = (bf16[4,256,256]{2,1,0:T(8,128)(2,1)}, bf16[4,1536,256]{2,1,0:T(8,128)(2,1)}, bf16[4,1536,256]{2,1,0:T(8,128)(2,1)}, bf16[4,256,256]{2,1,0:T(8,128)(2,...) custom-call(s32[16,1536]{1,0:T(8,128)} %get-tuple-element.135.send_i, ...), custom_call_target="tpu_custom_call" | custom-call | tf_op jit(solution)/shard_map/open/pallas_call | solution.py:817
  130.1 0.0 copy-done.4
  130.2 0.0 copy-start.61
  130.2 0.0 copy-start.64
  130.2 0.0 copy-start.77
  130.2 0.0 copy-start.95
  130.2 81.5 %close.1 = (bf16[4,1536,256]{2,1,0:T(8,128)(2,1)}, bf16[4,256,256]{2,1,0:T(8,128)(2,1)}, f32[3,256,256]{2,1,0:T(8,128)}) custom-call(bf16[4,256,256]{2,1,0:T(8,128)(2,1)S(1)} %copy-done.4, bf16[4,1536,256]{2,1,0:T(8,128)(2,1)} %edge_ref.3, bf16[4,1536,256]{2,1,0:T(8,128)(2,1)} %get-tuple-element.136.he_ref, bf16[4,1536,256]{2,1,0:T(8,128)(2,1)} %get-tuple-element.137.ye_ref, ...), custom_call_target="tpu_custom_call" | custom-call | tf_op jit(solution)/shard_map/close/pallas_call | solution.py:837
  211.7 0.0 copy-done.61
  211.7 0.0 copy-done.64
  211.8 0.0 copy-done.77
  211.8 0.0 copy-done.95
  211.8 0.3 while.13
  212.1 3.3 %adam.1 = (f32[2,96,256]{2,1,0:T(8,128)}, f32[2,32,256]{2,1,0:T(8,128)}, f32[2,64,256]{2,1,0:T(8,128)}, f32[2,32,256]{2,1,0:T(8,128)}, f32[2,4,32]{2,1,0:T(4,128...) custom-call(f32[3,256,256]{2,1,0:T(8,128)} %get-tuple-element.490, ...), custom_call_target="tpu_custom_call" | custom-call | tf_op jit(solution)/shard_map/adam/pallas_call | solution.py:882
  215.4 1.9 copy.527
  217.3 3.8 %copy.528 = bf16[4,1536,256]{2,1,0:T(8,128)(2,1)} copy(bf16[4,1536,256]{2,1,0:T(8,128)(2,1)} %get-tuple-element.492) | data formatting | bytes 6291456
Async XLA Ops:
  0.7 129.5 %copy-start.4 = (bf16[4,256,256]{2,1,0:T(8,128)(2,1)S(1)}, bf16[4,256,256]{2,1,0:T(8,128)(2,1)}, u32[]{:S(2)}) copy-start(bf16[4,256,256]{2,1,0:T(8,128)(2,1)} %nodes_ref.3) | copy-start | bytes 1572868
  130.2 81.6 %copy-start.61 = (f32[2,96,256]{2,1,0:T(8,128)S(1)}, f32[2,96,256]{2,1,0:T(8,128)}, u32[]{:S(2)}) copy-start(f32[2,96,256]{2,1,0:T(8,128)} %refs_0_.1) | copy-start | bytes 589828
  130.2 81.6 %copy-start.64 = (f32[2,64,256]{2,1,0:T(8,128)S(1)}, f32[2,64,256]{2,1,0:T(8,128)}, u32[]{:S(2)}) copy-start(f32[2,64,256]{2,1,0:T(8,128)} %refs_2_.1) | copy-start | bytes 393220
  130.2 81.6 %copy-start.77 = (s32[1536]{0:T(1024)S(1)}, s32[1536]{0:T(1024)}, u32[]{:S(2)}) copy-start(s32[1536]{0:T(1024)} %param.27) | copy-start | bytes 18436
  130.2 81.6 %copy-start.95 = (f32[2,4,32]{2,1,0:T(4,128)S(1)}, f32[2,4,32]{2,1,0:T(4,128)}, u32[]{:S(2)}) copy-start(f32[2,4,32]{2,1,0:T(4,128)} %refs_4_.1) | copy-start | bytes 3076

commit v2 on v1

--- a/solution.py
+++ b/solution.py
@@ -152,8 +152,12 @@
     return high, mid, low
 
 
+def to_f(cond):
+    return jnp.where(cond, 1.0, 0.0)
+
+
 def to_bf(cond):
-    return jnp.where(cond, 1.0, 0.0).astype(BF)
+    return to_f(cond).astype(BF)
 
 
 def onehot_cols(col_ids, first, width):
@@ -321,8 +325,8 @@
     is_me = row == me
     own_tile = jnp.sum(jnp.where(is_me, tile_of, 0), axis=0, keepdims=True)
     own_local = jnp.sum(jnp.where(is_me, local, 0.0), axis=0, keepdims=True)
-    own = jnp.where(own_tile == row, 1.0, 0.0)
-    inc = jnp.where((tile_of == me) & jnp.logical_not(is_me), 1.0, 0.0)
+    own = to_f(own_tile == row)
+    inc = to_f((tile_of == me) & jnp.logical_not(is_me))
     both = jnp.concatenate([own, inc], axis=0).astype(BF)
     rank = jnp.zeros((2 * tiles, edges), F32)
     step = 256
@@ -334,7 +338,7 @@
     gidx = jnp.sum(own * slot_id, axis=0, keepdims=True)
     grow_ref[...] = jnp.broadcast_to(gidx, grow_ref.shape).astype(jnp.int32)
     gcol_ref[...] = jnp.transpose(jnp.broadcast_to(gidx, (LANES, edges))).astype(jnp.int32)
-    mask = mask_ref[...].astype(F32)
+    mask = jnp.concatenate([mask_ref[line:line + 1, :] for line in range(mask_ref.shape[0])], axis=1).astype(F32)
     mrow_ref[...] = jnp.broadcast_to(mask, mrow_ref.shape)
     mcol_ref[...] = jnp.transpose(jnp.broadcast_to(mask, (LANES, edges)))
     slot_row = lax.broadcasted_iota(jnp.int32, (slots, edges), 0).astype(F32)
@@ -387,32 +391,30 @@
     return e_new, sums, branch_n, edge_s, node_s
 
 
-def ids_kernel(tiles, slots, tile_nodes, mine_ref, ids_ref, most_ref, wide, send_sem, recv_sem):
+def share_ids(peers, mine_ref, wide, ids_ref, most_ref, send_sem, recv_sem, tile_nodes):
     me = lax.axis_index('sp')
-    peers = tile_peers(tiles)
-    greet(peers)
     wide[me] = mine_ref[...]
-    greeted(len(peers))
     copies = [pltpu.make_async_remote_copy(src_ref=mine_ref, dst_ref=wide.at[me], send_sem=send_sem.at[spot], recv_sem=recv_sem.at[spot], device_id=peer, device_id_type=MESH_ID) for spot, peer in enumerate(peers)]
     for copy in copies:
         copy.start()
     for copy in copies:
         copy.wait()
-    for line in range(wide.shape[1]):
-        ids_ref[:, line * LANES:(line + 1) * LANES] = wide[:, line, :]
+    tiles, lines, lanes = wide.shape
+    for line in range(lines):
+        ids_ref[:, line * lanes:(line + 1) * lanes] = wide[:, line, :]
     tile_of = ids_ref[...] // tile_nodes
-    row = lax.broadcasted_iota(jnp.int32, (tiles, LANES), 0)
-    most = jnp.zeros((tiles, LANES), F32)
+    row = lax.broadcasted_iota(jnp.int32, (tiles, lanes), 0)
+    most = jnp.zeros((tiles, lanes), F32)
     for peer in range(tiles):
-        count = jnp.sum(jnp.where(tile_of == peer, 1.0, 0.0), axis=1, keepdims=True)
+        count = jnp.sum(to_f(tile_of == peer), axis=1, keepdims=True)
         most = jnp.maximum(most, jnp.where(row == peer, 0.0, count))
     most_ref[...] = jnp.broadcast_to(jnp.max(most, axis=0, keepdims=True), most_ref.shape)
 
 
-def open_kernel(cfg, shards, send_ids, mask_ref, nodes_ref, node_ref, edge_ref, dnode_ref, dedge_ref, m_e1, m_e2, m_n1, m_n2, m_norm,
-                vout_ref, he_ref, ye_ref, sum_ref, hn_ref, yn_ref, de_ref, dloc_ref, sloc_ref, grad_ref, grow_ref, nrow_ref, mcol_ref, mrow_ref, w_e1, w_e2, w_n1, w_n2, norm_ref, recv_out,
-                gcol_ref, pick_ref, drop_ref, pack_ref, rows_ref, dpre_ref, e_two, v_two, out_buf, in_buf, next_buf, in_two, part_ref, gat_ref,
-                send_a, recv_a, self_a, send_b, recv_b, self_b, send_c, recv_c, self_c, send_w, recv_w, self_w, send_x, recv_x, self_x):
+def open_kernel(cfg, shards, mine_ref, mask_ref, nodes_ref, node_ref, edge_ref, dnode_ref, dedge_ref, m_e1, m_e2, m_n1, m_n2, m_norm,
+                vout_ref, he_ref, ye_ref, sum_ref, hn_ref, yn_ref, de_ref, dloc_ref, sloc_ref, grad_ref, grow_ref, nrow_ref, mcol_ref, mrow_ref, w_e1, w_e2, w_n1, w_n2, norm_ref, most_ref, recv_out,
+                wide, ids_ref, gcol_ref, pick_ref, drop_ref, pack_ref, rows_ref, dpre_ref, e_two, v_two, out_buf, in_buf, next_buf, in_two, part_ref, gat_ref,
+                send_a, recv_a, self_a, send_b, recv_b, self_b, send_c, recv_c, self_c, send_w, recv_w, self_w, send_x, recv_x, self_x, send_i, recv_i):
     tiles, slots, tile_nodes, degree = cfg
     samples = nodes_ref.shape[0]
     all_wts = (w_e1, w_e2, w_n1, w_n2)
@@ -425,17 +427,25 @@
 
     @pl.when(step == 0)
     def _():
-        peers = tile_peers(tiles) + shard_peers(shards)
+        plane = tile_peers(tiles)
+        peers = plane + shard_peers(shards)
         greet(peers)
         cast_parts((m_e1, m_e2, m_n1, m_n2, m_norm), part_ref)
-        make_tables(tiles, slots, tile_nodes, send_ids, mask_ref, nodes_ref, gcol_ref, grow_ref, nrow_ref, mcol_ref, mrow_ref, pack_ref, out_buf)
         greeted(len(peers))
+        share_ids(plane, mine_ref, wide, ids_ref, most_ref, send_i, recv_i, tile_nodes)
+        make_tables(tiles, slots, tile_nodes, ids_ref, mask_ref, nodes_ref, gcol_ref, grow_ref, nrow_ref, mcol_ref, mrow_ref, pack_ref, out_buf)
         for sample in range(samples):
             slots_start(out_buf, in_buf, sample, send_a, recv_a, self_a, tiles)
         for layer, sems in enumerate(weight_sems):
             shards_start(part_ref.at[layer], gat_ref.at[layer], *sems, shards, False)
         build_pick(gcol_ref, pick_ref)
+        build_drop(grow_ref, drop_ref)
+        grad_ref[...] = jnp.zeros_like(grad_ref)
         take_weights(0)
+
+    @pl.when(step == samples - 1)
+    def _():
+        take_weights(1)
 
     @pl.when(step < samples)
     def _():
@@ -457,12 +467,6 @@
             return carry
         lax.fori_loop(0, tiles // 4, pack, 0)
         slots_start(next_buf, in_two, step, send_b, recv_b, self_b, tiles)
-
-    @pl.when(step == samples)
-    def _():
-        take_weights(1)
-        build_drop(grow_ref, drop_ref)
-        grad_ref[...] = jnp.zeros_like(grad_ref)
 
     @pl.when(step >= samples)
     def _():
@@ -661,10 +665,22 @@
         full_ref[shard, NORM_OFF + 8:, :] = jnp.zeros((rows_all - NORM_OFF - 8, width), F32)
 
 
-def adam_kernel(shards, both_ref, *refs):
-    refs, extra = refs[:-1], refs[-1]
+def adam_kernel(shards, both_ref, dnode_ref, dedge_ref, *refs):
+    count = (len(refs) - 7) // 2
+    node_out, edge_out = refs[count:count + 2]
+    refs = refs[:count] + refs[count + 2:]
+    extra, node_buf, edge_buf, sems_in, sems_out = refs[-5:]
+    moves = []
+    for k, (src, buf, dst) in enumerate(((dedge_ref, edge_buf, edge_out), (dnode_ref, node_buf, node_out))):
+        for sample in range(src.shape[0]):
+            moves.append((pltpu.make_async_copy(src.at[sample], buf.at[sample], sems_in.at[k, sample]), pltpu.make_async_copy(buf.at[sample], dst.at[sample], sems_out.at[k, sample])))
+    for load, store in moves:
+        load.start()
+    for load, store in moves:
+        load.wait()
+        store.start()
     dp = lax.axis_index('dp')
-    masters, ones, twos, new_masters, new_ones, new_twos = (refs[i:i + 5] for i in range(0, len(refs), 5))
+    masters, ones, twos, new_masters, new_ones, new_twos = (refs[i:i + 5] for i in range(0, len(refs) - 5, 5))
     layers, gains, lanes = masters[-1].shape
     norm = both_ref[:2, NORM_OFF:NORM_OFF + gains, :lanes]
     for shard in range(1, shards):
@@ -678,6 +694,8 @@
         results = adamw_update(masters[slot][...], grad_sum, ones[slot][...], twos[slot][...])
         for ref, value in zip((new_masters[slot], new_ones[slot], new_twos[slot]), results):
             ref[...] = value
+    for load, store in moves:
+        store.wait()
 
 
 def whole(shape):
@@ -773,7 +791,7 @@
         sums = tuple(jnp.stack([per_layer[slot] for per_layer in layer_grads], axis=0) for slot in range(5))
         return sums + (d_node, d_edge.reshape(edge_lat.shape))
 
-    def compact_step(node_lat, edge_lat, send_all, edge_mask, node_cot, edge_cot, masters):
+    def compact_step(node_lat, edge_lat, senders, edge_mask, node_cot, edge_cot, masters):
         samples, tile_nodes, width = node_lat.shape
         edges = edge_lat.shape[1]
         cfg = (tiles, SLOTS, tile_nodes, edges // tile_nodes)
@@ -800,6 +818,9 @@
         nrow_b = sd((8, tiles * SLOTS), jnp.int32)
         mcol_b = sd((edges, LANES), F32)
         mrow_b = sd((8, edges), F32)
+        lines = edges // LANES
+        most_b = sd((8, LANES), F32)
+        few = pltpu.SemaphoreType.DMA((tiles,))
         weights_b = [sd((layers, rows * dp_size, width), BF) for rows in SHARD_ROWS] + [sd((layers, 8, width), F32)]
 
         def full_specs(shapes):
@@ -816,23 +837,22 @@
         tables_b = [grow_b, nrow_b, mcol_b, mrow_b]
         outs = pl.pallas_call(
             functools.partial(open_kernel, cfg, dp_size), grid=(2 * samples,),
-            out_shape=[node_b, edge_b, edge_b, node_b, node_b, node_b, edge_b, node_f, node_f, grad_f] + tables_b + weights_b + [slot_b],
-            in_specs=[whole((tiles, edges)), whole((1, edges)), whole(node_b.shape), early(tile_nodes), early(edges), late(tile_nodes), late(edges)] + [whole(master.shape) for master in masters],
-            out_specs=[early(tile_nodes), early(edges), early(edges), early(tile_nodes), early(tile_nodes), early(tile_nodes), late(edges), late(tile_nodes), late(tile_nodes)] + full_specs([grad_f] + tables_b + weights_b) + [hbm],
-            scratch_shapes=[scratch(mcol_b.shape, jnp.int32), scratch((edges, cols)), drop_v, scratch((tiles * SLOTS, tile_nodes)), scratch((cols, width)), dpre_v, scratch(edge_b.shape), scratch(node_b.shape),
+            out_shape=[node_b, edge_b, edge_b, node_b, node_b, node_b, edge_b, node_f, node_f, grad_f] + tables_b + weights_b + [most_b, slot_b],
+            in_specs=[whole((lines, LANES)), whole((lines, LANES)), whole(node_b.shape), early(tile_nodes), early(edges), late(tile_nodes), late(edges)] + [whole(master.shape) for master in masters],
+            out_specs=[early(tile_nodes), early(edges), early(edges), early(tile_nodes), early(tile_nodes), early(tile_nodes), late(edges), late(tile_nodes), late(tile_nodes)] + full_specs([grad_f] + tables_b + weights_b + [most_b]) + [hbm],
+            scratch_shapes=[scratch((tiles, lines, LANES), jnp.int32), scratch((tiles, edges), jnp.int32), scratch(mcol_b.shape, jnp.int32), scratch((edges, cols)), drop_v, scratch((tiles * SLOTS, tile_nodes)), scratch((cols, width)), dpre_v, scratch(edge_b.shape), scratch(node_b.shape),
                             slot_v, slot_v, slot_v, slot_v, scratch((layers, PART_ROWS, width)), scratch((layers, dp_size, PART_ROWS, width))]
-            + slot_sems(samples, tiles) + slot_sems(samples, tiles) + slot_sems(samples, tiles) + shard_sems(dp_size) + shard_sems(dp_size),
-            name='open', compiler_params=remote_params(1))(send_all, edge_mask.reshape(1, edges), node_lat, node_lat, edge_lat, node_cot, edge_cot, *masters)
+            + slot_sems(samples, tiles) + slot_sems(samples, tiles) + slot_sems(samples, tiles) + shard_sems(dp_size) + shard_sems(dp_size) + [few, few],
+            name='open', compiler_params=remote_params(1))(senders.reshape(lines, LANES), edge_mask.reshape(lines, LANES), node_lat, node_lat, edge_lat, node_cot, edge_cot, *masters)
         v_one, h_e, y_e, sums, h_n, y_n, d_edge, d_loc, s_loc, grad_two, grow, nrow, mcol, mrow = outs[:14]
-        weights = outs[14:-1]
-        recv_three = outs[-1]
+        weights = outs[14:-2]
+        most, recv_three = outs[-2:]
 
         node_s = per_sample(tile_nodes, width)
         edge_s = per_sample(edges, width)
         rows = FULL_ROWS // tiles
         groups = layers + 1
         both_f = (groups, FULL_ROWS, width)
-        few = pltpu.SemaphoreType.DMA((tiles,))
         half_v = scratch((dp_size // 2, FULL_ROWS, width), F32)
         d_edge0, d_node, both = pl.pallas_call(
             functools.partial(close_kernel, cfg, dp_size), grid=(samples,),
@@ -843,7 +863,7 @@
                             half_v, half_v, scratch(both_f, F32), scratch((tiles, groups, rows, width), F32), scratch((groups, rows, width), F32), scratch((dp_size, rows, width), F32), scratch(both_f, F32)]
             + slot_sems(samples, tiles) + shard_sems(dp_size) + [few] * 12 + [pltpu.SemaphoreType.DMA],
             name='close', compiler_params=remote_params(2))(node_lat, edge_lat, h_e, y_e, sums, h_n, y_n, d_edge, node_lat, grow, mrow, mcol, nrow, *weights, v_one, d_loc, s_loc, recv_three, grad_two)
-        return both, d_node, d_edge0
+        return most[0, 0] <= SLOTS, both, d_node, d_edge0
 
     def general_both(*args):
         result = general_step(*args)
@@ -858,15 +878,8 @@
         moments_one = (mom_edge1, mom_edge2, mom_node1, mom_node2, mom_norm)
         moments_two = (vel_edge1, vel_edge2, vel_node1, vel_node2, vel_norm)
         tile_nodes = node_lat.shape[1]
-        lines = senders.shape[0] // LANES
         vmem = pl.BlockSpec(memory_space=pltpu.VMEM)
-        few = pltpu.SemaphoreType.DMA((tiles,))
-        send_all, most = pl.pallas_call(
-            functools.partial(ids_kernel, tiles, SLOTS, tile_nodes),
-            out_shape=(jax.ShapeDtypeStruct((tiles, lines * LANES), jnp.int32), jax.ShapeDtypeStruct((8, LANES), F32)),
-            in_specs=[vmem], out_specs=(vmem, vmem), scratch_shapes=[pltpu.VMEM((tiles, lines, LANES), jnp.int32), few, few],
-            name='ids', compiler_params=remote_params(0))(senders.reshape(lines, LANES))
-        fits = most[0, 0] <= SLOTS
+        hbm = pl.BlockSpec(memory_space=pl.ANY)
 
         def unsettled(state):
             return jnp.logical_not(state[0])
@@ -876,12 +889,17 @@
             args = (node_lat, edge_lat, senders, edge_mask, node_cot, edge_cot, held)
             return (True,) + jax.tree.map(row_major, general_both(*jax.tree.map(row_major, args)))
 
-        state = (fits,) + compact_step(node_lat, edge_lat, send_all, edge_mask, node_cot, edge_cot, masters)
+        state = compact_step(node_lat, edge_lat, senders, edge_mask, node_cot, edge_cot, masters)
         both, d_node, d_edge = lax.while_loop(unsettled, settle, state)[1:]
         state = masters + moments_one + moments_two
+        passed = [jax.ShapeDtypeStruct(item.shape, item.dtype) for item in (d_node, d_edge)]
+        width = w_edge2.shape[-1]
+        sems = pltpu.SemaphoreType.DMA((2, d_node.shape[0]))
         new_state = pl.pallas_call(
-            functools.partial(adam_kernel, dp_size), out_shape=[jax.ShapeDtypeStruct(item.shape, F32) for item in state],
-            in_specs=[vmem] * (len(state) + 1), out_specs=[vmem] * len(state), scratch_shapes=[pltpu.VMEM((w_edge2.shape[-1] * 3, w_edge2.shape[-1]), F32)], name='adam', compiler_params=pltpu.CompilerParams(**PARAMS))(both, *state)
-        return tuple(new_state) + (d_node, d_edge)
+            functools.partial(adam_kernel, dp_size), out_shape=passed + [jax.ShapeDtypeStruct(item.shape, F32) for item in state],
+            in_specs=[vmem, hbm, hbm] + [vmem] * len(state), out_specs=[hbm, hbm] + [vmem] * len(state),
+            scratch_shapes=[pltpu.VMEM((w_edge1.shape[1] * dp_size, width), F32), pltpu.VMEM(d_node.shape, BF), pltpu.VMEM(d_edge.shape, BF), sems, sems],
+            name='adam', compiler_params=pltpu.CompilerParams(**PARAMS))(both, d_node, d_edge, *state)
+        return tuple(new_state[2:]) + tuple(new_state[:2])
 
     return jax.shard_map(train_step, mesh=mesh, in_specs=(lat_spec, lat_spec, edge_spec, edge_spec, lat_spec, lat_spec) + param_specs + param_specs + param_specs, out_specs=param_specs + param_specs + param_specs + (lat_spec, lat_spec), check_vma=False)

time: 221 us -> 213 us (0.964)
  local copies, waits for them, and re-layouts: 8.2 us -> 1.22 us
    pallas_call x1, Pallas kernels: 114 us -> 125 us  [compact_step(): pl.pallas_call(functools.partial(open_kernel, cfg, dp_size), grid=(2 * sa...]
    pallas_call x2 -> x1, Pallas kernels: 15.5 us -> 5.86 us  [train_step(): pl.pallas_call(functools.partial(adam_kernel, dp_size), out_shape=passed...]
    unnamed x12 -> x10, local copies, waits for them, and re-layouts: 5.66 us -> 0.03 us
    pallas_call x1, Pallas kernels: 81.5 us -> 79.2 us  [compact_step(): pl.pallas_call(functools.partial(close_kernel, cfg, dp_size), grid=(sampl...]
where the time goes in v2:
time: 213 us
  Pallas kernels  210 us (99%)
    pallas_call x1, Pallas kernels, compact_step(): pl.pallas_call(functools.partial(open_kernel, cfg, dp_size), grid=(2 * sa...  125 us
    pallas_call x1, Pallas kernels, compact_step(): pl.pallas_call(functools.partial(close_kernel, cfg, dp_size), grid=(sampl...  79.2 us
    pallas_call x1, Pallas kernels, train_step(): pl.pallas_call(functools.partial(adam_kernel, dp_size), out_shape=passed...  5.86 us

profile of v2, /device:TPU:1, one launch (start us, length us, event | category | flops | bytes accessed | tf_op | source)
XLA Modules:
  0.0 212.7 jit_solution(11824502918408153074)
XLA Ops:
  0.7 0.0 copy-start.4
  0.7 124.5 %open.1 = (bf16[4,256,256]{2,1,0:T(8,128)(2,1)}, bf16[4,1536,256]{2,1,0:T(8,128)(2,1)}, bf16[4,1536,256]{2,1,0:T(8,128)(2,1)}, bf16[4,256,256]{2,1,0:T(8,128)(2,...) custom-call(s32[12,128]{1,0:T(8,128)} %bitcast.350, ...), custom_call_target="tpu_custom_call" | custom-call | tf_op jit(solution)/shard_map/open/pallas_call | solution.py:838
  125.2 1.2 slice.158
  127.0 0.0 copy-done.4
  127.1 0.0 copy-start.61
  127.1 0.0 copy-start.64
  127.1 0.0 copy-start.77
  127.1 0.0 copy-start.95
  127.1 79.2 %close.1 = (bf16[4,1536,256]{2,1,0:T(8,128)(2,1)}, bf16[4,256,256]{2,1,0:T(8,128)(2,1)}, f32[3,256,256]{2,1,0:T(8,128)}) custom-call(bf16[4,256,256]{2,1,0:T(8,128)(2,1)S(1)} %copy-done.4, bf16[4,1536,256]{2,1,0:T(8,128)(2,1)} %edge_ref.3, bf16[4,1536,256]{2,1,0:T(8,128)(2,1)} %get-tuple-element.136.he_ref, bf16[4,1536,256]{2,1,0:T(8,128)(2,1)} %get-tuple-element.137.ye_ref, ...), custom_call_target="tpu_custom_call" | custom-call | tf_op jit(solution)/shard_map/close/pallas_call | solution.py:857
  206.3 0.0 copy-done.61
  206.3 0.0 copy-done.64
  206.3 0.0 copy-done.77
  206.3 0.0 copy-done.95
  206.3 0.3 while.13
  206.6 5.9 %adam.1 = (bf16[4,256,256]{2,1,0:T(8,128)(2,1)}, bf16[4,1536,256]{2,1,0:T(8,128)(2,1)}, f32[2,96,256]{2,1,0:T(8,128)}, f32[2,32,256]{2,1,0:T(8,128)}, f32[2,64,2...) custom-call(f32[3,256,256]{2,1,0:T(8,128)} %get-tuple-element.458, ...), custom_call_target="tpu_custom_call" | custom-call | tf_op jit(solution)/shard_map/adam/pallas_call | solution.py:898
Async XLA Ops:
  0.7 126.4 %copy-start.4 = (bf16[4,256,256]{2,1,0:T(8,128)(2,1)S(1)}, bf16[4,256,256]{2,1,0:T(8,128)(2,1)}, u32[]{:S(2)}) copy-start(bf16[4,256,256]{2,1,0:T(8,128)(2,1)} %nodes_ref.3) | copy-start | bytes 1572868
  127.1 79.2 %copy-start.61 = (f32[2,96,256]{2,1,0:T(8,128)S(1)}, f32[2,96,256]{2,1,0:T(8,128)}, u32[]{:S(2)}) copy-start(f32[2,96,256]{2,1,0:T(8,128)} %refs_0_.1) | copy-start | bytes 589828
  127.1 79.2 %copy-start.64 = (f32[2,64,256]{2,1,0:T(8,128)S(1)}, f32[2,64,256]{2,1,0:T(8,128)}, u32[]{:S(2)}) copy-start(f32[2,64,256]{2,1,0:T(8,128)} %refs_2_.1) | copy-start | bytes 393220
  127.1 79.2 %copy-start.77 = (s32[1536]{0:T(1024)S(1)}, s32[1536]{0:T(1024)}, u32[]{:S(2)}) copy-start(s32[1536]{0:T(1024)} %param.27) | copy-start | bytes 18436
  127.1 79.2 %copy-start.95 = (f32[2,4,32]{2,1,0:T(4,128)S(1)}, f32[2,4,32]{2,1,0:T(4,128)}, u32[]{:S(2)}) copy-start(f32[2,4,32]{2,1,0:T(4,128)} %refs_4_.1) | copy-start | bytes 3076

commit v3 on v2

--- a/solution.py
+++ b/solution.py
@@ -21,6 +21,7 @@
 BF = jnp.bfloat16
 F32 = jnp.float32
 SLOTS = 80
+LIVE = 72
 MESH_ID = pl.DeviceIdType.MESH
 
 
@@ -249,22 +250,28 @@
     return [(peer_tile(me, offset, side), dp) for offset in far_first(tiles)]
 
 
-def slot_copy(src_ref, dst_ref, sample, spot, send_sem, recv_sem, peer, me):
-    return pltpu.make_async_remote_copy(src_ref=src_ref.at[peer[0], sample], dst_ref=dst_ref.at[me, sample], send_sem=send_sem.at[sample, spot], recv_sem=recv_sem.at[sample, spot], device_id=peer, device_id_type=MESH_ID)
-
-
-def slots_start(src_ref, dst_ref, sample, send_sem, recv_sem, self_sem, tiles):
+def slot_copy(src_ref, dst_ref, sample, spot, send_sem, recv_sem, peer, me, live):
+    rows = pl.ds(0, live)
+    return pltpu.make_async_remote_copy(src_ref=src_ref.at[peer[0], sample, rows], dst_ref=dst_ref.at[me, sample, rows], send_sem=send_sem.at[sample, spot], recv_sem=recv_sem.at[sample, spot], device_id=peer, device_id_type=MESH_ID)
+
+
+def clear_spare(ref):
+    first = LIVE // 16 * 16
+    ref[:, :, first:, :] = jnp.zeros(ref.shape[:2] + (ref.shape[2] - first, ref.shape[3]), BF)
+
+
+def slots_start(src_ref, dst_ref, sample, send_sem, recv_sem, self_sem, tiles, live=SLOTS):
     me = lax.axis_index('sp')
     pltpu.make_async_copy(src_ref.at[me, sample], dst_ref.at[me, sample], self_sem.at[sample]).start()
     for spot, peer in enumerate(tile_peers(tiles)):
-        slot_copy(src_ref, dst_ref, sample, spot, send_sem, recv_sem, peer, me).start()
-
-
-def slots_wait(src_ref, dst_ref, sample, send_sem, recv_sem, self_sem, tiles):
+        slot_copy(src_ref, dst_ref, sample, spot, send_sem, recv_sem, peer, me, live).start()
+
+
+def slots_wait(src_ref, dst_ref, sample, send_sem, recv_sem, self_sem, tiles, live=SLOTS):
     me = lax.axis_index('sp')
     pltpu.make_async_copy(src_ref.at[me, sample], dst_ref.at[me, sample], self_sem.at[sample]).wait()
     for spot, peer in enumerate(tile_peers(tiles)):
-        slot_copy(src_ref, dst_ref, sample, spot, send_sem, recv_sem, peer, me).wait()
+        slot_copy(src_ref, dst_ref, sample, spot, send_sem, recv_sem, peer, me, live).wait()
 
 
 def slots_wait_all(src_ref, dst_ref, samples, send_sem, recv_sem, self_sem, tiles):
@@ -315,7 +322,7 @@
     return out
 
 
-def make_tables(tiles, slots, tile_nodes, send_ids, mask_ref, node_ref, gcol_ref, grow_ref, nrow_ref, mcol_ref, mrow_ref, pack_ref, out_ref):
+def make_tables(tiles, slots, tile_nodes, send_ids, mask_ref, gcol_ref, grow_ref, nrow_ref, mcol_ref, mrow_ref, pack_ref):
     me = lax.axis_index('sp')
     ids = send_ids[...]
     edges = ids.shape[1]
@@ -350,14 +357,17 @@
     ncol_f = jnp.concatenate(cols, axis=0)
     ncol = ncol_f.astype(jnp.int32)
     nrow_ref[...] = jnp.transpose(ncol_f)[:8].astype(jnp.int32)
-    group = 4
-    for part in range(tiles // group):
-        rows = group * slots
-        pick = onehot_cols(ncol[part * rows:(part + 1) * rows], 0, tile_nodes)
-        pack_ref[part * rows:(part + 1) * rows, :] = pick
-        for sample in range(out_ref.shape[1]):
-            got = dot_nn(pick, node_ref[sample]).astype(BF)
-            out_ref[part * group:(part + 1) * group, sample] = got.reshape(group, slots, got.shape[1])
+    pack_ref[...] = onehot_cols(ncol, 0, tile_nodes)
+
+
+def pack_sample(sample, node, pack_ref, out_ref, tiles, slots):
+    def pack(i, carry):
+        rows = 4 * slots
+        base = pl.multiple_of(i * rows, rows)
+        got = dot_nn(pack_ref[pl.ds(base, rows), :], node).astype(BF)
+        out_ref[pl.ds(i * 4, 4), sample] = got.reshape(4, slots, got.shape[1])
+        return carry
+    lax.fori_loop(0, tiles // 4, pack, 0)
 
 
 def fill_rows(rows_ref, node, got, tile_nodes):
@@ -429,13 +439,15 @@
     def _():
         plane = tile_peers(tiles)
         peers = plane + shard_peers(shards)
+        clear_spare(in_buf)
         greet(peers)
         cast_parts((m_e1, m_e2, m_n1, m_n2, m_norm), part_ref)
         greeted(len(peers))
         share_ids(plane, mine_ref, wide, ids_ref, most_ref, send_i, recv_i, tile_nodes)
-        make_tables(tiles, slots, tile_nodes, ids_ref, mask_ref, nodes_ref, gcol_ref, grow_ref, nrow_ref, mcol_ref, mrow_ref, pack_ref, out_buf)
+        make_tables(tiles, slots, tile_nodes, ids_ref, mask_ref, gcol_ref, grow_ref, nrow_ref, mcol_ref, mrow_ref, pack_ref)
         for sample in range(samples):
-            slots_start(out_buf, in_buf, sample, send_a, recv_a, self_a, tiles)
+            pack_sample(sample, nodes_ref[sample], pack_ref, out_buf, tiles, slots)
+            slots_start(out_buf, in_buf, sample, send_a, recv_a, self_a, tiles, LIVE)
         for layer, sems in enumerate(weight_sems):
             shards_start(part_ref.at[layer], gat_ref.at[layer], *sems, shards, False)
         build_pick(gcol_ref, pick_ref)
@@ -449,7 +461,7 @@
 
     @pl.when(step < samples)
     def _():
-        slots_wait(out_buf, in_buf, step, send_a, recv_a, self_a, tiles)
+        slots_wait(out_buf, in_buf, step, send_a, recv_a, self_a, tiles, LIVE)
         fill_rows(rows_ref, node_ref[0], in_buf[:, step], tile_nodes)
         node, edge = node_ref[0], edge_ref[0]
         e_new, sums, branch_n, edge_s, node_s = fwd_sample(chunk_maps(degree, mrow_ref[...], None), node, edge, pick_ref, rows_ref, [ref.at[0] for ref in all_wts], norm_ref.at[0])
@@ -458,14 +470,7 @@
             ref[0] = value
         e_two[step] = e_new
         v_two[step] = v_new
-
-        def pack(i, carry):
-            rows = 4 * slots
-            base = pl.multiple_of(i * rows, rows)
-            got = dot_nn(pack_ref[pl.ds(base, rows), :], vout_ref[0]).astype(BF)
-            next_buf[pl.ds(i * 4, 4), step] = got.reshape(4, slots, got.shape[1])
-            return carry
-        lax.fori_loop(0, tiles // 4, pack, 0)
+        pack_sample(step, v_new, pack_ref, next_buf, tiles, slots)
         slots_start(next_buf, in_two, step, send_b, recv_b, self_b, tiles)
 
     @pl.when(step >= samples)
@@ -554,6 +559,7 @@
 
     @pl.when(step == 0)
     def _():
+        clear_spare(in_buf)
         greet(plane + others)
         fold_ref[...] = onehot_rows(nrow_ref[:1], 0, tile_nodes)
         gsend_ref[...] = jnp.zeros_like(gsend_ref)
@@ -573,7 +579,7 @@
     node_s = again(hn_ref[0], yn_ref[0])
     back_sample(maps, node_ref[0], edge_ref[0], sum_ref[0], edge_s, node_s, dv_ref[step].astype(F32), dedge_ref, [ref.at[0] for ref in (w_e1, w_e2, w_n1, w_n2)], norms_ref.at[0], grad_ref, dpre_ref, de_ref, dloc_ref.at[pl.ds(step, 1)])
     back_pack(dpre_ref, drop_ref, sloc_ref.at[pl.ds(step, 1)], send_buf, step, tiles, slots, tile_nodes)
-    slots_start(send_buf, in_buf, step, send_b, recv_b, self_b, tiles)
+    slots_start(send_buf, in_buf, step, send_b, recv_b, self_b, tiles, LIVE)
 
     @pl.when(step == samples - 1)
     def _():
@@ -597,7 +603,7 @@
         pair[-1].wait()
 
         def finish(sample, carry):
-            slots_wait(send_buf, in_buf, sample, send_b, recv_b, self_b, tiles)
+            slots_wait(send_buf, in_buf, sample, send_b, recv_b, self_b, tiles, LIVE)
             dv_out[sample] = finish_sample(nodes_ref[sample], dloc_ref[sample], sloc_ref[sample], in_buf[:, sample], fold_ref, gsend_ref, w_e1.at[0])
             return carry
         lax.fori_loop(0, samples, finish, 0)
@@ -863,7 +869,7 @@
                             half_v, half_v, scratch(both_f, F32), scratch((tiles, groups, rows, width), F32), scratch((groups, rows, width), F32), scratch((dp_size, rows, width), F32), scratch(both_f, F32)]
             + slot_sems(samples, tiles) + shard_sems(dp_size) + [few] * 12 + [pltpu.SemaphoreType.DMA],
             name='close', compiler_params=remote_params(2))(node_lat, edge_lat, h_e, y_e, sums, h_n, y_n, d_edge, node_lat, grow, mrow, mcol, nrow, *weights, v_one, d_loc, s_loc, recv_three, grad_two)
-        return most[0, 0] <= SLOTS, both, d_node, d_edge0
+        return most[0, 0] <= LIVE, both, d_node, d_edge0
 
     def general_both(*args):
         result = general_step(*args)

time: 213 us -> 209 us (0.981)
  Pallas kernels: 210 us -> 205 us
    pallas_call x1, Pallas kernels: 125 us -> 120 us  [compact_step(): pl.pallas_call(functools.partial(open_kernel, cfg, dp_size), grid=(2 * sa...]
where the time goes in v3:
time: 209 us; the launch traced here: 208 us
  Pallas kernels  205 us (98%)
    pallas_call x1, Pallas kernels, compact_step(): pl.pallas_call(functools.partial(open_kernel, cfg, dp_size), grid=(2 * sa...  120 us
    pallas_call x1, Pallas kernels, compact_step(): pl.pallas_call(functools.partial(close_kernel, cfg, dp_size), grid=(sampl...  78.9 us
    pallas_call x1, Pallas kernels, train_step(): pl.pallas_call(functools.partial(adam_kernel, dp_size), out_shape=passed...  5.86 us

profile of v3, /device:TPU:1, one launch (start us, length us, event | category | flops | bytes accessed | tf_op | source)
XLA Modules:
  0.0 207.7 jit_solution(9721910089654315368)
XLA Ops:
  0.7 0.0 copy-start.4
  0.7 119.9 %open.1 = (bf16[4,256,256]{2,1,0:T(8,128)(2,1)}, bf16[4,1536,256]{2,1,0:T(8,128)(2,1)}, bf16[4,1536,256]{2,1,0:T(8,128)(2,1)}, bf16[4,256,256]{2,1,0:T(8,128)(2,...) custom-call(s32[12,128]{1,0:T(8,128)} %bitcast.350, ...), custom_call_target="tpu_custom_call" | custom-call | tf_op jit(solution)/shard_map/open/pallas_call | solution.py:844
  120.6 1.2 slice.158
  122.4 0.0 copy-done.4
  122.4 0.0 copy-start.61
  122.5 0.0 copy-start.64
  122.5 0.0 copy-start.77
  122.5 0.0 copy-start.95
  122.5 78.9 %close.1 = (bf16[4,1536,256]{2,1,0:T(8,128)(2,1)}, bf16[4,256,256]{2,1,0:T(8,128)(2,1)}, f32[3,256,256]{2,1,0:T(8,128)}) custom-call(bf16[4,256,256]{2,1,0:T(8,128)(2,1)S(1)} %copy-done.4, bf16[4,1536,256]{2,1,0:T(8,128)(2,1)} %edge_ref.3, bf16[4,1536,256]{2,1,0:T(8,128)(2,1)} %get-tuple-element.136.he_ref, bf16[4,1536,256]{2,1,0:T(8,128)(2,1)} %get-tuple-element.137.ye_ref, ...), custom_call_target="tpu_custom_call" | custom-call | tf_op jit(solution)/shard_map/close/pallas_call | solution.py:863
  201.4 0.0 copy-done.61
  201.4 0.0 copy-done.64
  201.4 0.0 copy-done.77
  201.4 0.0 copy-done.95
  201.4 0.3 while.13
  201.7 5.9 %adam.1 = (bf16[4,256,256]{2,1,0:T(8,128)(2,1)}, bf16[4,1536,256]{2,1,0:T(8,128)(2,1)}, f32[2,96,256]{2,1,0:T(8,128)}, f32[2,32,256]{2,1,0:T(8,128)}, f32[2,64,2...) custom-call(f32[3,256,256]{2,1,0:T(8,128)} %get-tuple-element.458, ...), custom_call_target="tpu_custom_call" | custom-call | tf_op jit(solution)/shard_map/adam/pallas_call | solution.py:904
Async XLA Ops:
  0.7 121.8 %copy-start.4 = (bf16[4,256,256]{2,1,0:T(8,128)(2,1)S(1)}, bf16[4,256,256]{2,1,0:T(8,128)(2,1)}, u32[]{:S(2)}) copy-start(bf16[4,256,256]{2,1,0:T(8,128)(2,1)} %nodes_ref.3) | copy-start | bytes 1572868
  122.4 78.9 %copy-start.61 = (f32[2,96,256]{2,1,0:T(8,128)S(1)}, f32[2,96,256]{2,1,0:T(8,128)}, u32[]{:S(2)}) copy-start(f32[2,96,256]{2,1,0:T(8,128)} %refs_0_.1) | copy-start | bytes 589828
  122.5 78.9 %copy-start.64 = (f32[2,64,256]{2,1,0:T(8,128)S(1)}, f32[2,64,256]{2,1,0:T(8,128)}, u32[]{:S(2)}) copy-start(f32[2,64,256]{2,1,0:T(8,128)} %refs_2_.1) | copy-start | bytes 393220
  122.5 78.9 %copy-start.77 = (s32[1536]{0:T(1024)S(1)}, s32[1536]{0:T(1024)}, u32[]{:S(2)}) copy-start(s32[1536]{0:T(1024)} %param.27) | copy-start | bytes 18436
  122.5 78.9 %copy-start.95 = (f32[2,4,32]{2,1,0:T(4,128)S(1)}, f32[2,4,32]{2,1,0:T(4,128)}, u32[]{:S(2)}) copy-start(f32[2,4,32]{2,1,0:T(4,128)} %refs_4_.1) | copy-start | bytes 3076
